TPU v7x, 32 devices: a whole 2x2x4 slice. The times are simulated.
32 devices in a mesh: dp: 2 (over x), t: 4 (over z), stage: 4 (over y, core).
Axes of the slice: x: 2, y: 2, z: 4, core: 2. Of those that a mesh axis runs over, the one named last changes fastest.
Arguments:
- hidden: bfloat16 [8, 4, 128, 7168], P(('dp', 'stage')), parts along dimension 0
- w_query: bfloat16 [7168, 24576], P(None, 't')
- w_dkv: bfloat16 [7168, 576], replicated
- latent_gain: bfloat16 [512], replicated
- w_uk: bfloat16 [512, 16384], P(None, 't')
- w_uv: bfloat16 [512, 16384], P(None, 't')
- w_out: bfloat16 [16384, 7168], P('t')
Outputs:
- output 1: bfloat16 [8, 4, 128, 7168], P(('dp', 'stage')), parts along dimension 0
- output 2: bfloat16 [8, 4, 128, 576], P(('dp', 'stage'), 't'), parts along dimension 0
There are 2 independent parts. A program takes and returns all parts, laid end to end along the dimension named above; an argument that names none is the same for every part.
All inputs are finite; a program needn't handle non-finite values.
Results may differ from a plain program's by a relative error of at most 0.010829.
Values are sent between devices in bfloat16 or wider.
A program may use at most 1 GiB of HBM per device.

v0:
```python
import jax
import jax.numpy as jnp
from jax import lax
from jax.sharding import PartitionSpec as P

NOPE_DIM = 128
ROPE_DIM = 64
V_DIM = 128
NORM_EPS = 1e-6
ROPE_BASE = 10000.0


def rope_tables(seq_len):
    half_dim = ROPE_DIM // 2
    positions = jnp.arange(seq_len, dtype=jnp.float32)
    inv_freq = ROPE_BASE ** (-jnp.arange(half_dim, dtype=jnp.float32) / half_dim)
    angles = positions[:, None] * inv_freq[None, :]
    return jnp.cos(angles), jnp.sin(angles)


def apply_rope(vecs, cos_tab, sin_tab):
    half_dim = vecs.shape[-1] // 2
    as_f32 = vecs.astype(jnp.float32)
    low_half = as_f32[..., :half_dim]
    high_half = as_f32[..., half_dim:]
    rotated = jnp.concatenate([low_half * cos_tab - high_half * sin_tab, high_half * cos_tab + low_half * sin_tab], axis=-1)
    return rotated.astype(jnp.bfloat16)


def latent_rows(tokens, w_dkv, latent_gain, cos_tab, sin_tab):
    kv_rank = latent_gain.shape[0]
    compressed = jnp.einsum("bsd,dc->bsc", tokens, w_dkv, preferred_element_type=jnp.float32).astype(jnp.bfloat16)
    c_raw = compressed[..., :kv_rank].astype(jnp.float32)
    inv_rms = lax.rsqrt(jnp.mean(c_raw * c_raw, axis=-1, keepdims=True) + NORM_EPS)
    c_kv = (c_raw * inv_rms * latent_gain.astype(jnp.float32)).astype(jnp.bfloat16)
    k_rope = apply_rope(compressed[..., kv_rank:], cos_tab, sin_tab)
    return jnp.concatenate([c_kv, k_rope], axis=-1)


def causal_heads(q_nope, q_rope, k_nope, k_rope, values):
    seq_len = q_nope.shape[1]
    n_blocks = max(1, min(8, seq_len // 128))
    block_len = seq_len // n_blocks
    score_scale = (q_nope.shape[-1] + q_rope.shape[-1]) ** -0.5
    pieces = []
    for block_idx in range(n_blocks):
        start_row = block_idx * block_len
        stop_row = start_row + block_len
        scores = jnp.einsum("bqhe,bkhe->bhqk", q_nope[:, start_row:stop_row], k_nope[:, :stop_row], preferred_element_type=jnp.float32)
        scores = scores + jnp.einsum("bqhe,bke->bhqk", q_rope[:, start_row:stop_row], k_rope[:, :stop_row], preferred_element_type=jnp.float32)
        q_pos = start_row + jnp.arange(block_len)[:, None]
        k_pos = jnp.arange(stop_row)[None, :]
        scores = jnp.where(k_pos <= q_pos, scores * score_scale, -jnp.inf)
        row_peak = jnp.max(scores, axis=-1, keepdims=True)
        weights = jnp.exp(scores - row_peak)
        row_total = jnp.sum(weights, axis=-1)
        mixed = jnp.einsum("bhqk,bkhe->bqhe", weights.astype(jnp.bfloat16), values[:, :stop_row], preferred_element_type=jnp.float32)
        pieces.append((mixed / jnp.transpose(row_total, (0, 2, 1))[..., None]).astype(jnp.bfloat16))
    return jnp.concatenate(pieces, axis=1)


def attention_partial(tokens, latent, w_query, w_uk, w_uv, w_out, cos_tab, sin_tab):
    kv_rank = w_uk.shape[0]
    batch, seq_len = tokens.shape[0], tokens.shape[1]
    heads_here = w_uk.shape[1] // NOPE_DIM
    queries = jnp.einsum("bsd,dn->bsn", tokens, w_query, preferred_element_type=jnp.float32).astype(jnp.bfloat16)
    queries = queries.reshape(batch, seq_len, heads_here, NOPE_DIM + ROPE_DIM)
    q_rope = apply_rope(queries[..., NOPE_DIM:], cos_tab[:, None, :], sin_tab[:, None, :])
    k_nope = jnp.einsum("bsr,rn->bsn", latent[..., :kv_rank], w_uk, preferred_element_type=jnp.float32).astype(jnp.bfloat16)
    k_nope = k_nope.reshape(batch, seq_len, heads_here, NOPE_DIM)
    values = jnp.einsum("bsr,rn->bsn", latent[..., :kv_rank], w_uv, preferred_element_type=jnp.float32).astype(jnp.bfloat16)
    values = values.reshape(batch, seq_len, heads_here, V_DIM)
    head_mix = causal_heads(queries[..., :NOPE_DIM], q_rope, k_nope, latent[..., kv_rank:], values)
    head_mix = head_mix.reshape(batch, seq_len, heads_here * V_DIM)
    return jnp.einsum("bsn,nd->bsd", head_mix, w_out, preferred_element_type=jnp.float32)


def solution(mesh):
    n_tp = mesh.shape["t"]
    half_stage = mesh.shape["stage"] // 2
    hand_pairs = [(source_idx, source_idx + half_stage) for source_idx in range(half_stage)]
    slot_spec = P(("dp", "stage"), None, None, None)
    cache_spec = P(("dp", "stage"), "t", None, None)

    def device_step(hidden, w_query, w_dkv, latent_gain, w_uk, w_uv, w_out):
        tokens = hidden[0]
        local_rows = tokens.shape[0] // n_tp
        t_index = lax.axis_index("t")
        cos_tab, sin_tab = rope_tables(tokens.shape[1])
        my_tokens = lax.dynamic_slice_in_dim(tokens, t_index * local_rows, local_rows, axis=0)
        my_latent = latent_rows(my_tokens, w_dkv, latent_gain, cos_tab, sin_tab)
        all_latent = lax.all_gather(my_latent, "t", axis=0, tiled=True)
        handed = lax.ppermute(my_latent, "stage", hand_pairs)
        part_sum = attention_partial(tokens, all_latent, w_query, w_uk, w_uv, w_out, cos_tab, sin_tab)
        summed = lax.psum(part_sum.astype(jnp.bfloat16), "t")
        is_prompt = lax.axis_index("stage") < half_stage
        out_rows = jnp.where(is_prompt, summed, jnp.zeros_like(summed))
        return out_rows[None], handed[None]

    return jax.shard_map(device_step, mesh=mesh, in_specs=(slot_spec, P(None, "t"), P(None, None), P(None), P(None, "t"), P(None, "t"), P("t", None)), out_specs=(slot_spec, cache_spec), check_vma=False)
```

profile of v0, /device:TPU:0, one launch (start us, length us, event | category | flops | bytes accessed | tf_op | source)
XLA Modules:
  0.0 437.5 jit_solution(5381148847164458604)
XLA Ops:
  7.2 0.0 all-reduce.2.cloned.1.call-start
  7.2 0.0 copy-start.4
  7.2 0.0 copy-start.3
  7.3 6.3 %fusion.39 = bf16[1,128,576]{1,2,0:T(8,128)(2,1)S(1)} fusion(bf16[7168,576]{0,1:T(8,128)(2,1)} %param.9, bf16[1,4,128,7168]{3,2,1,0:T(8,128)(2,1)} %param.7, s32[]{:T(128)S(6)} %select_n.16), kind=kOutput, calls=%fused_computation.37 | convolution fusion | flops 1057038336 | bytes 10240004 | tf_op jit(solution)/shard_map/bsd,dc->bsc/dot_general | solution.py:32
  13.6 0.1 fusion.44
  13.7 0.1 fusion.48
  13.9 0.1 subtract_convert_fusion.1
  14.0 0.0 copy-done.4
  14.0 0.1 fusion.46
  14.2 18.8 %all_gather.3 = bf16[4,128,576]{1,2,0:T(8,128)(2,1)S(1)} all-gather(bf16[1,128,576]{1,2,0:T(8,128)(2,1)S(1)} %pad_maximum_fusion), channel_id=1, replica_groups=mesh['dp'=2,'t'=4,'stage'=4] {'t'}, dimensions={0}, use_global_device_ids=true | all-gather | bytes 737280 | tf_op jit(solution)/shard_map/all_gather | solution.py:92
  33.0 0.0 copy-done.3
  33.0 52.7 %fusion.7 = bf16[4,128,6144]{2,1,0:T(8,128)(2,1)} fusion(bf16[7168,6144]{1,0:T(8,128)(2,1)} %param.8, bf16[1,4,128,7168]{3,2,1,0:T(8,128)(2,1)S(1)} %copy-done.3), kind=kOutput, calls=%fused_computation.5 | convolution fusion | flops 45100302336 | bytes 101711872 | tf_op jit(solution)/shard_map/bsd,dn->bsn/dot_general | solution.py:66
  85.7 8.6 %copy.26 = bf16[4,128,6144]{1,2,0:T(8,128)(2,1)} copy(bf16[4,128,6144]{2,1,0:T(8,128)(2,1)} %fusion.7) | data formatting | bytes 12582912 | tf_op jit(solution)/shard_map/convert_element_type | solution.py:66
  94.3 0.0 copy-start
  94.3 0.0 slice-start
  94.3 4.4 slice_convert_fusion
  98.7 0.0 copy-done
  98.7 0.0 slice-start.1
  98.7 2.4 fusion.27
  101.1 0.0 slice-done
  101.1 0.0 slice-done.1
  101.1 0.0 copy-start.1
  101.1 4.5 %fusion.18 = f32[4,32,128,128]{2,3,1,0:T(8,128)} fusion(bf16[4,16,32,8,128]{4,3,2,1,0:T(8,128)(2,1)S(1)} %fusion.27, bf16[4,128,32,192]{1,3,2,0:T(8,128)(2,1)S(1)} %bitcast.65), kind=kOutput, calls=%fused_computation.19 | convolution fusion | flops 536870912 | bytes 16777216 | tf_op jit(solution)/shard_map/bqhe,bkhe->bhqk/dot_general | solution.py:49
  105.6 0.0 copy-done.1
  105.6 4.3 convolution_convert_fusion.1
  109.9 6.3 %copy.35 = bf16[4,128,4096]{1,2,0:T(8,128)(2,1)} copy(bf16[4,128,4096]{2,1,0:T(8,128)(2,1)} %convolution_convert_fusion.1) | data formatting | bytes 8388608 | tf_op jit(solution)/shard_map/reshape | solution.py:72
  116.2 2.8 subtract_convert_fusion
  119.0 4.6 %fusion.53 = (f32[4,32,128]{2,1,0:T(8,128)S(1)}, f32[4,32,128,128]{2,3,1,0:T(8,128)S(1)}) fusion(f32[4,32,128,128]{2,3,1,0:T(8,128)} %fusion.18, bf16[4,128,32,32]{1,3,2,0:T(8,128)(2,1)S(1)} %get-tuple-element.3, bf16[4,128,32,32]{1,3,2,0:T(8,128)(2,1)S(1)} %get-tuple-element.2, bf16[4,128,576]{1,2,0:T(8,128)(2,1)S(1)} %all_gather.3, ...), kind=kOutput, calls=%fused_computation.61 | convolution fusion | flops 281001984 | bytes 19021824 | tf_op jit(solution)/shard_map/bqhe,bke->bhqk/dot_general | solution.py:50
  123.6 0.0 copy-start.2
  123.6 2.3 fusion.13
  125.9 0.0 copy-done.2
  125.9 2.3 fusion.10
  128.3 38.4 %fusion.4 = bf16[4,128,7168]{2,1,0:T(8,128)(2,1)} fusion(bf16[4,128,4096]{1,2,0:T(8,128)(2,1)S(1)} %bitcast.69, bf16[4096,7168]{1,0:T(8,128)(2,1)} %param.13), kind=kOutput, calls=%fused_computation.4 | convolution fusion | flops 30068441088 | bytes 70254592 | tf_op jit(solution)/shard_map/bsn,nd->bsd/dot_general | solution.py:75
  166.7 0.0 all-reduce.2.cloned.1.call-update
  166.7 3.4 collective-permute-start
  170.1 2.6 collective-permute-done
  172.8 250.6 %all-reduce.2.cloned.1.call-done = bf16[4,128,7168]{2,1,0:T(8,128)(2,1)} async-done(((bf16[4,128,7168]{2,1,0:T(8,128)(2,1)}), bf16[4,128,7168]{2,1,0:T(8,128)(2,1)}) %all-reduce.2.cloned.1.call-update) | async-done | bytes 7340048 | tf_op jit(solution)/shard_map/psum | solution.py:95
  423.4 6.6 %select_bitcast_fusion = bf16[1,4,128,7168]{3,2,1,0:T(8,128)(2,1)} fusion(bf16[4,128,7168]{2,1,0:T(8,128)(2,1)} %all-reduce.2.cloned.1.call-done, pred[]{:T(512)S(6)} %lt.6), kind=kLoop, calls=%fused_computation.15 | loop fusion | flops 3670016 | bytes 14680065 | tf_op jit(solution)/shard_map/broadcast_in_dim | solution.py:98
  430.0 0.7 copy.45
  (7 shorter events, 0.1 us)
Async XLA Ops:
  7.2 416.3 %all-reduce.2.cloned.1.call-start = ((), (), s32[]{:S(2)}) async-start(), calls=%async_computation | async-start | bytes 14680064 | tf_op jit(solution)/shard_map/psum | solution.py:95
  7.2 6.8 %copy-start.4 = (bf16[512]{0:T(512)(128)(2,1)S(1)}, bf16[512]{0:T(512)(128)(2,1)}, u32[]{:S(2)}) copy-start(bf16[512]{0:T(512)(128)(2,1)} %param.10) | copy-start | bytes 3076
  7.2 25.8 %copy-start.3 = (bf16[1,4,128,7168]{3,2,1,0:T(8,128)(2,1)S(1)}, bf16[1,4,128,7168]{3,2,1,0:T(8,128)(2,1)}, u32[]{:S(2)}) copy-start(bf16[1,4,128,7168]{3,2,1,0:T(8,128)(2,1)} %param.7) | copy-start | bytes 22020100
  94.3 4.4 copy-start
  94.3 6.8 %slice-start = ((s8[6291456]{0:T(1024)(128)(4,1)}), s8[4194304]{0:T(1024)(128)(4,1)S(1)}, s32[]{:S(2)}) async-start(s8[6291456]{0:T(1024)(128)(4,1)} %bitcast.63), calls=%async_computation.1 | async-start | bytes 8388608
  98.7 2.4 slice-start.1
  101.1 4.5 %copy-start.1 = (bf16[512,4096]{1,0:T(8,128)(2,1)S(1)}, bf16[512,4096]{1,0:T(8,128)(2,1)}, u32[]{:S(2)}) copy-start(bf16[512,4096]{1,0:T(8,128)(2,1)} %param.12) | copy-start | bytes 12582916
  123.6 2.3 copy-start.2
  166.7 6.1 %collective-permute-start = (bf16[1,128,576]{1,2,0:T(8,128)(2,1)S(1)}, bf16[1,128,576]{1,2,0:T(8,128)(2,1)S(1)}, u32[]{:S(2)}, u32[]{:S(2)}) collective-permute-start(bf16[1,128,576]{1,2,0:T(8,128)(2,1)S(1)} %pad_maximum_fusion), channel_id=1, source_target_pairs={{0,2},{1,3},{4,6},{5,7},{8,10},{9,11},{12,14},{13,15},{16,18},{17,... | collective-permute-start | bytes 442376 | tf_op jit(solution)/shard_map/ppermute | solution.py:93
Sparse Core Ops, SparseCore 0:
  166.8 256.5 all-reduce.1
where the time goes:
time: 438 us
  waiting for transfers between devices  253 us (58%)
  matrix products  116 us (26%)
  blocking collectives  18.8 us (4%)
  other arithmetic  16.6 us (4%)
  local copies, waits for them, and re-layouts  15.6 us (4%)
  between operations  14.2 us (3%)
    psum x1, waiting for transfers between devices, device_step(): summed = lax.psum(part_sum.astype(jnp.bfloat16), 't')  251 us
    dot_general x1, matrix products, attention_partial(): jnp.einsum('bsd,dn->bsn', tokens, w_query, preferred_element_type=jnp.flo...  52.7 us
    dot_general x1, matrix products, attention_partial(): jnp.einsum('bsn,nd->bsd', head_mix, w_out, preferred_element_type=jnp.flo...  38.4 us
    all_gather x1, blocking collectives, device_step(): all_latent = lax.all_gather(my_latent, 't', axis=0, tiled=True)  18.8 us
  transfers between devices with their start and end apart: 2, of which 2 were waited for; matrix products, arithmetic and copies ran while one was open for 0% of the time, Pallas kernels for 0%

commit v1 on v0

--- a/solution.py
+++ b/solution.py
@@ -1,6 +1,10 @@
+import functools
+
 import jax
 import jax.numpy as jnp
 from jax import lax
+from jax.experimental import pallas as pl
+from jax.experimental.pallas import tpu as pltpu
 from jax.sharding import PartitionSpec as P
 
 NOPE_DIM = 128
@@ -8,6 +12,9 @@
 V_DIM = 128
 NORM_EPS = 1e-6
 ROPE_BASE = 10000.0
+MESH = pl.DeviceIdType.MESH
+TILE = 256
+HOP_LAG = 2
 
 
 def rope_tables(seq_len):
@@ -59,7 +66,7 @@
     return jnp.concatenate(pieces, axis=1)
 
 
-def attention_partial(tokens, latent, w_query, w_uk, w_uv, w_out, cos_tab, sin_tab):
+def head_outputs(tokens, latent, w_query, w_uk, w_uv, cos_tab, sin_tab):
     kv_rank = w_uk.shape[0]
     batch, seq_len = tokens.shape[0], tokens.shape[1]
     heads_here = w_uk.shape[1] // NOPE_DIM
@@ -71,30 +78,214 @@
     values = jnp.einsum("bsr,rn->bsn", latent[..., :kv_rank], w_uv, preferred_element_type=jnp.float32).astype(jnp.bfloat16)
     values = values.reshape(batch, seq_len, heads_here, V_DIM)
     head_mix = causal_heads(queries[..., :NOPE_DIM], q_rope, k_nope, latent[..., kv_rank:], values)
-    head_mix = head_mix.reshape(batch, seq_len, heads_here * V_DIM)
-    return jnp.einsum("bsn,nd->bsd", head_mix, w_out, preferred_element_type=jnp.float32)
+    return head_mix.reshape(batch * seq_len, heads_here * V_DIM)
+
+
+def project_reduce_kernel(n_tiles, n_steps, o_ref, w_ref, lat_ref, out_ref, cache_ref, part, partb, ebuf, ibuf,
+                          send_b, recv_p, send_e, recv_e, send_i, recv_i, send_f, send_o, recv_o, local_sem, lat_sem):
+    step = pl.program_id(0)
+    t = lax.axis_index("t")
+    stage = lax.axis_index("stage")
+    is_prompt = stage < 2
+    is_relay = stage >= 2
+    partner = lax.rem(stage + 2, 4)
+    is_end = (t == 0) | (t == 3)
+    is_inner = (t == 1) | (t == 2)
+    peer = 3 - t
+    inner_nb = jnp.where(t == 0, 1, 2)
+    end_nb = jnp.where(t == 1, 0, 3)
+    half = part.shape[1]
+    seq = cache_ref.shape[0]
+
+    def to_partner(j):
+        return pltpu.make_async_remote_copy(src_ref=partb.at[j], dst_ref=part.at[j], send_sem=send_b.at[j], recv_sem=recv_p.at[j],
+                                            device_id={"stage": partner}, device_id_type=MESH)
+
+    def end_to_inner(j):
+        return pltpu.make_async_remote_copy(src_ref=part.at[j], dst_ref=ebuf.at[j], send_sem=send_e.at[j], recv_sem=recv_e.at[j],
+                                            device_id={"t": inner_nb}, device_id_type=MESH)
+
+    def inner_to_peer(j):
+        return pltpu.make_async_remote_copy(src_ref=part.at[j], dst_ref=ibuf.at[j], send_sem=send_i.at[j], recv_sem=recv_i.at[j],
+                                            device_id={"t": peer}, device_id_type=MESH)
+
+    def final_to_end(j, src):
+        return pltpu.make_async_remote_copy(src_ref=src.at[j], dst_ref=ibuf.at[j], send_sem=send_f.at[j], recv_sem=recv_i.at[j],
+                                            device_id={"t": end_nb}, device_id_type=MESH)
+
+    def cols(j):
+        return pl.ds(pl.multiple_of(j * TILE, TILE), TILE)
+
+    def final_back(j, src):
+        return pltpu.make_async_remote_copy(src_ref=src.at[j], dst_ref=out_ref.at[pl.ds(half, half), cols(j)], send_sem=send_o.at[j],
+                                            recv_sem=recv_o.at[j], device_id={"stage": partner}, device_id_type=MESH)
+
+    def final_local(j, src):
+        return pltpu.make_async_copy(src.at[j], out_ref.at[pl.ds(0, half), cols(j)], local_sem.at[j])
+
+    def cache_copy():
+        return pltpu.make_async_remote_copy(src_ref=lat_ref.at[pl.ds(pl.multiple_of(t * seq, seq), seq)], dst_ref=cache_ref, send_sem=lat_sem.at[0],
+                                            recv_sem=lat_sem.at[1], device_id={"stage": partner}, device_id_type=MESH)
+
+    def deliver(j, src):
+        @pl.when(is_prompt)
+        def _():
+            final_local(j, src).start()
+
+        @pl.when(is_relay)
+        def _():
+            final_back(j, src).start()
+
+    def live(j):
+        return (j >= 0) & (j < n_tiles)
+
+    @pl.when(step == 0)
+    def _():
+        barrier = pltpu.get_barrier_semaphore()
+        pl.semaphore_signal(barrier, inc=1, device_id={"stage": partner}, device_id_type=MESH)
+
+        @pl.when(is_end)
+        def _():
+            pl.semaphore_signal(barrier, inc=1, device_id={"t": inner_nb}, device_id_type=MESH)
+            pl.semaphore_wait(barrier, 2)
+
+        @pl.when(is_inner)
+        def _():
+            pl.semaphore_signal(barrier, inc=1, device_id={"t": end_nb}, device_id_type=MESH)
+            pl.semaphore_signal(barrier, inc=1, device_id={"t": peer}, device_id_type=MESH)
+            pl.semaphore_wait(barrier, 3)
+
+        @pl.when(is_prompt)
+        def _():
+            cache_copy().start()
+
+    @pl.when(is_prompt & (step < n_tiles))
+    def _():
+        full = jnp.dot(o_ref[...], w_ref[...], preferred_element_type=jnp.float32).astype(jnp.bfloat16)
+        part[step] = full[:half]
+        partb[step] = full[half:]
+        to_partner(step).start()
+
+    own = step - jnp.where(is_relay, HOP_LAG, 0)
+
+    @pl.when(is_relay & live(own))
+    def _():
+        to_partner(own).wait_recv()
+
+    @pl.when(is_end & live(own))
+    def _():
+        end_to_inner(own).start()
+
+    first = own - HOP_LAG
+    root_first = 1 + lax.rem(first + 2 * n_tiles, 2)
+
+    @pl.when(is_inner & live(first))
+    def _():
+        end_to_inner(first).wait_recv()
+
+        @pl.when(t != root_first)
+        def _():
+            part[first] = (part[first].astype(jnp.float32) + ebuf[first].astype(jnp.float32)).astype(jnp.bfloat16)
+            inner_to_peer(first).start()
+
+    second = first - HOP_LAG
+    root_second = 1 + lax.rem(second + 2 * n_tiles, 2)
+
+    @pl.when(is_inner & live(second) & (t == root_second))
+    def _():
+        inner_to_peer(second).wait_recv()
+        total = part[second].astype(jnp.float32) + ebuf[second].astype(jnp.float32) + ibuf[second].astype(jnp.float32)
+        part[second] = total.astype(jnp.bfloat16)
+        inner_to_peer(second).start()
+        final_to_end(second, part).start()
+        deliver(second, part)
+
+    third = second - HOP_LAG
+    root_third = 1 + lax.rem(third + 2 * n_tiles, 2)
+
+    @pl.when(is_inner & live(third) & (t != root_third))
+    def _():
+        inner_to_peer(third).wait_recv()
+        final_to_end(third, ibuf).start()
+        deliver(third, ibuf)
+
+    fourth = third - HOP_LAG
+
+    @pl.when(is_end & live(fourth))
+    def _():
+        final_to_end(fourth, ibuf).wait_recv()
+        deliver(fourth, ibuf)
+
+    @pl.when(step == n_steps - 1)
+    def _():
+        @pl.loop(0, n_tiles)
+        def _(j):
+            @pl.when(is_end)
+            def _():
+                end_to_inner(j).wait_send()
+
+            @pl.when(is_inner)
+            def _():
+                inner_to_peer(j).wait_send()
+                final_to_end(j, part).wait_send()
+
+            @pl.when(is_prompt)
+            def _():
+                to_partner(j).wait_send()
+                final_local(j, part).wait()
+                final_back(j, part).wait_recv()
+
+            @pl.when(is_relay)
+            def _():
+                final_back(j, part).wait_send()
+
+        @pl.when(is_prompt)
+        def _():
+            cache_copy().wait_send()
+
+        @pl.when(is_relay)
+        def _():
+            cache_copy().wait_recv()
+
+
+def project_reduce(head_mix, w_out, latent, seq_len):
+    rows, depth = head_mix.shape
+    width = w_out.shape[1]
+    n_tiles = width // TILE
+    n_steps = n_tiles + 5 * HOP_LAG
+    half = rows // 2
+    any_spec = pl.BlockSpec(memory_space=pl.ANY)
+    chunk = pltpu.VMEM((n_tiles, half, TILE), jnp.bfloat16)
+    return pl.pallas_call(
+        functools.partial(project_reduce_kernel, n_tiles, n_steps),
+        grid=(n_steps,),
+        out_shape=(jax.ShapeDtypeStruct((rows, width), jnp.bfloat16), jax.ShapeDtypeStruct((seq_len, latent.shape[1]), jnp.bfloat16)),
+        in_specs=[
+            pl.BlockSpec((rows, depth), lambda i: (0, 0)),
+            pl.BlockSpec((depth, TILE), lambda i: (0, jnp.minimum(i, n_tiles - 1))),
+            any_spec,
+        ],
+        out_specs=(any_spec, any_spec),
+        scratch_shapes=[chunk, chunk, chunk, chunk] + [pltpu.SemaphoreType.DMA((n_tiles,))] * 10 + [pltpu.SemaphoreType.DMA((2,))],
+        compiler_params=pltpu.CompilerParams(collective_id=0, has_side_effects=True, vmem_limit_bytes=56 * 1024 * 1024),
+    )(head_mix, w_out, latent)
 
 
 def solution(mesh):
-    n_tp = mesh.shape["t"]
     half_stage = mesh.shape["stage"] // 2
-    hand_pairs = [(source_idx, source_idx + half_stage) for source_idx in range(half_stage)]
     slot_spec = P(("dp", "stage"), None, None, None)
     cache_spec = P(("dp", "stage"), "t", None, None)
 
     def device_step(hidden, w_query, w_dkv, latent_gain, w_uk, w_uv, w_out):
         tokens = hidden[0]
-        local_rows = tokens.shape[0] // n_tp
-        t_index = lax.axis_index("t")
-        cos_tab, sin_tab = rope_tables(tokens.shape[1])
-        my_tokens = lax.dynamic_slice_in_dim(tokens, t_index * local_rows, local_rows, axis=0)
-        my_latent = latent_rows(my_tokens, w_dkv, latent_gain, cos_tab, sin_tab)
-        all_latent = lax.all_gather(my_latent, "t", axis=0, tiled=True)
-        handed = lax.ppermute(my_latent, "stage", hand_pairs)
-        part_sum = attention_partial(tokens, all_latent, w_query, w_uk, w_uv, w_out, cos_tab, sin_tab)
-        summed = lax.psum(part_sum.astype(jnp.bfloat16), "t")
+        batch, seq_len, width = tokens.shape
+        cos_tab, sin_tab = rope_tables(seq_len)
+        latent = latent_rows(tokens, w_dkv, latent_gain, cos_tab, sin_tab)
+        head_mix = head_outputs(tokens, latent, w_query, w_uk, w_uv, cos_tab, sin_tab)
+        summed, handed = project_reduce(head_mix, w_out, latent.reshape(batch * seq_len, -1), seq_len)
         is_prompt = lax.axis_index("stage") < half_stage
-        out_rows = jnp.where(is_prompt, summed, jnp.zeros_like(summed))
-        return out_rows[None], handed[None]
+        out_rows = jnp.where(is_prompt, summed, jnp.zeros_like(summed)).reshape(batch, seq_len, width)
+        cache = jnp.where(is_prompt, jnp.zeros_like(handed), handed)
+        return out_rows[None], cache[None, None]
 
     return jax.shard_map(device_step, mesh=mesh, in_specs=(slot_spec, P(None, "t"), P(None, None), P(None), P(None, "t"), P(None, "t"), P("t", None)), out_specs=(slot_spec, cache_spec), check_vma=False)

time: 438 us -> 255 us (0.58)
  waiting for transfers between devices: 253 us -> 0 us
  Pallas kernels: 0 us -> 120 us
  matrix products: 116 us -> 85.1 us
  local copies, waits for them, and re-layouts: 15.6 us -> 36.3 us
  blocking collectives: 18.8 us -> 0 us
  between operations: 14.2 us -> 0.82 us
  other arithmetic: 16.6 us -> 11.9 us
    psum x1 -> x0, waiting for transfers between devices: 251 us -> none  [device_step(): summed = lax.psum(part_sum.astype(jnp.bfloat16), 't')]
    pallas_call x0 -> x1, Pallas kernels: none -> 120 us  [project_reduce(): pl.pallas_call(functools.partial(project_reduce_kernel, n_tiles, n_steps)...]
    dot_general x4 -> x3, matrix products: 97.8 us -> 61.5 us  [the longest x1 52.7 us: head_outputs(): jnp.einsum('bsd,dn->bsn', tokens, w_query, preferred_element_type=jnp.flo...]
    all_gather x1 -> x0, blocking collectives: 18.8 us -> none  [device_step(): all_latent = lax.all_gather(my_latent, 't', axis=0, tiled=True)]
    unnamed x15 -> x14, local copies, waits for them, and re-layouts: 0.69 us -> 12.3 us
    convert_element_type x1 -> x2, local copies, waits for them, and re-layouts: 8.61 us -> 16.5 us  [the longest x1 8.65 us: head_outputs(): jnp.einsum('bsd,dn->bsn', tokens, w_query, preferred_element_type=jnp.flo...]
    select_n x0 -> x1, other arithmetic: none -> 6.65 us  [device_step(): jnp.where(is_prompt, summed, jnp.zeros_like(summed))]
    dot_general x1, matrix products: 2.32 us -> 8.97 us  [causal_heads(): jnp.einsum('bhqk,bkhe->bqhe', weights.astype(jnp.bfloat16), values[:, :st...]
  transfers between devices with their start and end apart: 2 -> 0, of which waited for: 2 -> 0; matrix products, arithmetic and copies ran while one was open for 0% -> 0% of each run, Pallas kernels for 0% -> 0%
where the time goes in v1:
time: 255 us; the launch traced here: 254 us
  Pallas kernels  120 us (47%)
  matrix products  85.1 us (33%)
  local copies, waits for them, and re-layouts  36.3 us (14%)
  other arithmetic  11.9 us (5%)
    pallas_call x1, Pallas kernels, project_reduce(): pl.pallas_call(functools.partial(project_reduce_kernel, n_tiles, n_steps)...  120 us
    dot_general x1, matrix products, head_outputs(): jnp.einsum('bsd,dn->bsn', tokens, w_query, preferred_element_type=jnp.flo...  52.7 us
    unnamed x14, local copies, waits for them, and re-layouts  12.3 us
    dot_general x1, matrix products, causal_heads(): jnp.einsum('bhqk,bkhe->bqhe', weights.astype(jnp.bfloat16), values[:, :st...  8.97 us
    convert_element_type x1, local copies, waits for them, and re-layouts, head_outputs(): jnp.einsum('bsd,dn->bsn', tokens, w_query, preferred_element_type=jnp.flo...  8.65 us
    dot_general x1, matrix products, latent_rows(): jnp.einsum('bsd,dc->bsc', tokens, w_dkv, preferred_element_type=jnp.float32)  8.18 us
    convert_element_type x1, local copies, waits for them, and re-layouts, causal_heads(): (mixed / jnp.transpose(row_total, (0, 2, 1))[..., None]).astype(jnp.bfloa...  7.88 us
    select_n x1, other arithmetic, device_step(): jnp.where(is_prompt, summed, jnp.zeros_like(summed))  6.65 us

profile of v1, /device:TPU:0, one launch (start us, length us, event | category | flops | bytes accessed | tf_op | source)
XLA Modules:
  0.0 253.6 jit_solution(14300223194606801019)
XLA Ops:
  0.6 0.0 copy-start.4
  0.6 0.0 copy-start.1
  0.7 8.2 %fusion.31 = bf16[4,128,576]{1,2,0:T(8,128)(2,1)S(1)} fusion(bf16[7168,576]{0,1:T(8,128)(2,1)} %param.9, bf16[1,4,128,7168]{3,2,1,0:T(8,128)(2,1)} %param.7), kind=kOutput, calls=%fused_computation.34 | convolution fusion | flops 4228153344 | bytes 16187392 | tf_op jit(solution)/shard_map/bsd,dc->bsc/dot_general | solution.py:39
  8.9 0.1 fusion.42
  9.1 0.1 fusion.36
  9.2 0.0 copy-done.4
  9.2 0.2 fusion.38
  9.4 0.0 copy-done.1
  9.4 0.0 copy-start.5
  9.4 4.5 %fusion.25 = bf16[4,16,32,8,128]{4,3,2,1,0:T(8,128)(2,1)} fusion(bf16[4,128,512]{1,2,0:T(8,128)(2,1)S(1)} %fusion.38, bf16[512,4096]{1,0:T(8,128)(2,1)S(1)} %copy-done.1), kind=kOutput, calls=%fused_computation.27 | convolution fusion | flops 2149580800 | bytes 8912896 | tf_op jit(solution)/shard_map/bsr,rn->bsn/dot_general | solution.py:76
  13.9 0.0 copy-done.5
  13.9 52.7 %fusion.2 = bf16[4,128,6144]{2,1,0:T(8,128)(2,1)} fusion(bf16[7168,6144]{1,0:T(8,128)(2,1)} %param.8, bf16[1,4,128,7168]{3,2,1,0:T(8,128)(2,1)S(1)} %copy-done.5), kind=kOutput, calls=%fused_computation.2 | convolution fusion | flops 45100302336 | bytes 101711872 | tf_op jit(solution)/shard_map/bsd,dn->bsn/dot_general | solution.py:73
  66.6 8.6 %copy.20 = bf16[4,128,6144]{1,2,0:T(8,128)(2,1)} copy(bf16[4,128,6144]{2,1,0:T(8,128)(2,1)} %fusion.2) | data formatting | bytes 12582912 | tf_op jit(solution)/shard_map/convert_element_type | solution.py:73
  75.2 4.7 %fusion.16 = f32[4,32,128,128]{2,3,1,0:T(8,128)S(1)} fusion(bf16[4,16,32,8,128]{4,3,2,1,0:T(8,128)(2,1)} %fusion.25, bf16[4,128,32,192]{1,3,2,0:T(8,128)(2,1)} %bitcast.62), kind=kOutput, calls=%fused_computation.20 | convolution fusion | flops 536870912 | bytes 16777216 | tf_op jit(solution)/shard_map/bqhe,bkhe->bhqk/dot_general | solution.py:56
  80.0 2.0 slice_convert_fusion
  82.0 0.6 subtract_convert_fusion
  82.6 1.6 fusion.44
  84.3 0.0 copy-start
  84.3 0.0 copy-start.2
  84.3 2.0 fusion.10
  86.3 2.2 copy-done
  88.5 1.0 copy-done.2
  89.5 4.4 %convolution_convert_fusion.1 = bf16[4,128,4096]{2,1,0:T(8,128)(2,1)} fusion(bf16[4,128,512]{1,2,0:T(8,128)(2,1)S(1)} %fusion.38, bf16[512,4096]{1,0:T(8,128)(2,1)S(1)} %copy-done.2), kind=kOutput, calls=%fused_computation.17 | convolution fusion | flops 2149580800 | bytes 8912896 | tf_op jit(solution)/shard_map/bsr,rn->bsn/dot_general | solution.py:78
  93.9 6.3 %copy.33 = bf16[4,128,4096]{1,2,0:T(8,128)(2,1)} copy(bf16[4,128,4096]{2,1,0:T(8,128)(2,1)} %convolution_convert_fusion.1) | data formatting | bytes 8388608 | tf_op jit(solution)/shard_map/reshape | solution.py:79
  100.2 9.0 %fusion.5 = bf16[4,128,32,128]{1,3,2,0:T(8,128)(2,1)} fusion(f32[4,128,32]{1,2,0:T(8,128)S(1)} %bitcast.69, bf16[4,128,32,128]{1,3,2,0:T(8,128)(2,1)} %bitcast.67, f32[4,32,128,128]{2,3,1,0:T(8,128)} %copy-done, f32[4,32,128]{2,1,0:T(8,128)S(1)} %get-tuple-element.16), kind=kOutput, calls=%fused_computation.4 | convolution fusion | flops 545259520 | bytes 16908288 | tf_op jit(solution)/shard_map/bhqk,bkhe->bqhe/dot_general | solution.py:64
  109.2 7.9 %copy.26 = bf16[4,128,32,128]{3,2,1,0:T(8,128)(2,1)} copy(bf16[4,128,32,128]{1,3,2,0:T(8,128)(2,1)} %fusion.5) | data formatting | bytes 8388608 | tf_op jit(solution)/shard_map/convert_element_type | solution.py:65
  117.1 8.4 %copy.42 = bf16[64,8,32,128]{3,1,2,0:T(8,128)(2,1)} copy(bf16[64,8,32,128]{3,2,1,0:T(8,128)(2,1)} %bitcast.64) | data formatting | bytes 8388608
  125.5 1.1 copy.27
  126.6 119.6 %shard_map.86 = (bf16[512,7168]{1,0:T(8,128)(2,1)}, bf16[128,576]{1,0:T(8,128)(2,1)}) custom-call(bf16[512,4096]{1,0:T(8,128)(2,1)} %bitcast.65, bf16[4096,7168]{1,0:T(8,128)(2,1)} %w_ref.1, bf16[512,576]{1,0:T(8,128)(2,1)} %bitcast.68), custom_call_target="tpu_custom_call" | custom-call | tf_op jit(solution)/shard_map/pallas_call | solution.py:259
  246.1 0.0 copy-start.3
  246.2 6.7 %broadcast_select_fusion = bf16[512,7168]{1,0:T(8,128)(2,1)} fusion(bf16[512,7168]{1,0:T(8,128)(2,1)} %get-tuple-element.4, pred[]{:T(512)S(6)} %lt.3), kind=kLoop, calls=%fused_computation.15 | loop fusion | flops 3670016 | bytes 14680065 | tf_op jit(solution)/shard_map/jit(_where)/select_n | solution.py:287
  252.8 0.0 copy-done.3
  252.8 0.8 copy.28
  (8 shorter events, 0.1 us)
Async XLA Ops:
  0.6 8.6 %copy-start.4 = (bf16[512]{0:T(512)(128)(2,1)S(1)}, bf16[512]{0:T(512)(128)(2,1)}, u32[]{:S(2)}) copy-start(bf16[512]{0:T(512)(128)(2,1)} %param.10) | copy-start | bytes 3076
  0.6 8.8 %copy-start.1 = (bf16[512,4096]{1,0:T(8,128)(2,1)S(1)}, bf16[512,4096]{1,0:T(8,128)(2,1)}, u32[]{:S(2)}) copy-start(bf16[512,4096]{1,0:T(8,128)(2,1)} %param.11) | copy-start | bytes 12582916
  9.4 4.5 %copy-start.5 = (bf16[1,4,128,7168]{3,2,1,0:T(8,128)(2,1)S(1)}, bf16[1,4,128,7168]{3,2,1,0:T(8,128)(2,1)}, u32[]{:S(2)}) copy-start(bf16[1,4,128,7168]{3,2,1,0:T(8,128)(2,1)} %param.7) | copy-start | bytes 22020100
  84.3 4.3 %copy-start = (f32[4,32,128,128]{2,3,1,0:T(8,128)}, f32[4,32,128,128]{2,3,1,0:T(8,128)S(1)}, u32[]{:S(2)}) copy-start(f32[4,32,128,128]{2,3,1,0:T(8,128)S(1)} %get-tuple-element.17) | copy-start | bytes 25165828
  84.3 5.2 %copy-start.2 = (bf16[512,4096]{1,0:T(8,128)(2,1)S(1)}, bf16[512,4096]{1,0:T(8,128)(2,1)}, u32[]{:S(2)}) copy-start(bf16[512,4096]{1,0:T(8,128)(2,1)} %param.12) | copy-start | bytes 12582916
  246.1 6.7 %copy-start.3 = (bf16[128,576]{1,0:T(8,128)(2,1)S(1)}, bf16[128,576]{1,0:T(8,128)(2,1)}, u32[]{:S(2)}) copy-start(bf16[128,576]{1,0:T(8,128)(2,1)} %get-tuple-element.5) | copy-start | bytes 442372

commit v2 on v0

v2 whole, which is shorter than its diff:
```python
import functools

import jax
import jax.numpy as jnp
import numpy as np
from jax import lax
from jax.experimental import pallas as pl
from jax.experimental.pallas import tpu as pltpu
from jax.sharding import PartitionSpec as P

NOPE_DIM = 128
ROPE_DIM = 64
V_DIM = 128
NORM_EPS = 1e-6
ROPE_BASE = 10000.0
MESH = pl.DeviceIdType.MESH
TILE = 512
HOP_LAG = 2
HEADS_STEP = 4
PIECE = 16


def rope_tables(seq_len):
    half_dim = ROPE_DIM // 2
    positions = jnp.arange(seq_len, dtype=jnp.float32)
    inv_freq = ROPE_BASE ** (-jnp.arange(half_dim, dtype=jnp.float32) / half_dim)
    angles = positions[:, None] * inv_freq[None, :]
    return jnp.cos(angles), jnp.sin(angles)


def apply_rope(vecs, cos_tab, sin_tab):
    half_dim = vecs.shape[-1] // 2
    as_f32 = vecs.astype(jnp.float32)
    low_half = as_f32[..., :half_dim]
    high_half = as_f32[..., half_dim:]
    rotated = jnp.concatenate([low_half * cos_tab - high_half * sin_tab, high_half * cos_tab + low_half * sin_tab], axis=-1)
    return rotated.astype(jnp.bfloat16)


def latent_rows(tokens, w_dkv, latent_gain, cos_tab, sin_tab):
    kv_rank = latent_gain.shape[0]
    compressed = jnp.einsum("bsd,dc->bsc", tokens, w_dkv, preferred_element_type=jnp.float32).astype(jnp.bfloat16)
    c_raw = compressed[..., :kv_rank].astype(jnp.float32)
    inv_rms = lax.rsqrt(jnp.mean(c_raw * c_raw, axis=-1, keepdims=True) + NORM_EPS)
    c_kv = (c_raw * inv_rms * latent_gain.astype(jnp.float32)).astype(jnp.bfloat16)
    k_rope = apply_rope(compressed[..., kv_rank:], cos_tab, sin_tab)
    return jnp.concatenate([c_kv, k_rope], axis=-1)


def lane_tables(seq_len):
    half_dim = ROPE_DIM // 2
    inv_freq = np.float32(ROPE_BASE) ** (-np.arange(half_dim, dtype=np.float32) / np.float32(half_dim))
    angles = np.arange(seq_len, dtype=np.float32)[:, None] * inv_freq[None, :].astype(np.float32)
    cos_tab, sin_tab = np.cos(angles).astype(np.float32), np.sin(angles).astype(np.float32)
    one, zero = np.ones((seq_len, ROPE_DIM), np.float32), np.zeros((seq_len, ROPE_DIM), np.float32)
    cos_low = np.concatenate([cos_tab, cos_tab, one], axis=1)
    sin_low = np.concatenate([-sin_tab, sin_tab, zero], axis=1)
    cos_high = np.concatenate([one, cos_tab, cos_tab], axis=1)
    sin_high = np.concatenate([zero, -sin_tab, sin_tab], axis=1)
    return cos_low, sin_low, cos_high, sin_high


def rope_lanes(vecs, cos_tab, sin_tab, pick_up):
    as_f32 = vecs.astype(jnp.float32)
    turned = jnp.where(pick_up, pltpu.roll(as_f32, 96, 1), pltpu.roll(as_f32, 32, 1))
    return (as_f32 * cos_tab + turned * sin_tab).astype(jnp.bfloat16)


def project_heads(rows, slot, x_ref, wq_ref, wuk_ref, wuv_ref, lat_ref, q_buf, k_buf, v_buf):
    kv_rank = wuk_ref.shape[0]
    q_buf[slot, :rows] = jnp.dot(x_ref[:rows], wq_ref[...], preferred_element_type=jnp.float32).astype(jnp.bfloat16)
    c_kv = lat_ref[:rows, :kv_rank]
    k_buf[slot, :rows] = jnp.dot(c_kv, wuk_ref[...], preferred_element_type=jnp.float32).astype(jnp.bfloat16)
    v_buf[slot, :rows] = jnp.dot(c_kv, wuv_ref[...], preferred_element_type=jnp.float32).astype(jnp.bfloat16)


def attend_request(q_ref, k_ref, v_ref, lat_ref, tabs, here, seq):
    kv_rank = lat_ref.shape[1] - 128
    cos_low, sin_low, cos_high, sin_high = (tab[...] for tab in tabs)
    lane = lax.broadcasted_iota(jnp.int32, (seq, 128), 1)
    low = lane < 64
    pick_up = (lane & 32) == 0
    key_rope = lat_ref[here, kv_rank:]
    key_rope_high = pltpu.roll(key_rope.astype(jnp.float32), 64, 1)
    causal = lax.broadcasted_iota(jnp.int32, (seq, seq), 1) <= lax.broadcasted_iota(jnp.int32, (seq, seq), 0)
    scale = (NOPE_DIM + ROPE_DIM) ** -0.5
    all_scores = []
    for pair in range(HEADS_STEP // 2):
        base = 384 * pair
        q_a = q_ref[here, base:base + 128]
        q_b = rope_lanes(q_ref[here, base + 128:base + 256], cos_low, sin_low, pick_up)
        q_c = rope_lanes(q_ref[here, base + 256:base + 384], cos_high, sin_high, pick_up)
        k_even = k_ref[here, 256 * pair:256 * pair + 128]
        k_odd = pltpu.roll(k_ref[here, 256 * pair + 128:256 * pair + 256].astype(jnp.float32), 64, 1)
        k_odd_a = jnp.where(low, 0.0, k_odd).astype(jnp.bfloat16)
        k_odd_b = jnp.where(low, k_odd, key_rope_high).astype(jnp.bfloat16)
        sides = ((jnp.concatenate([q_a, q_b], axis=1), jnp.concatenate([k_even, key_rope], axis=1)),
                 (jnp.concatenate([q_b, q_c], axis=1), jnp.concatenate([k_odd_a, k_odd_b], axis=1)))
        for q_side, k_side in sides:
            all_scores.append(lax.dot_general(q_side, k_side, (((1,), (1,)), ((), ())), preferred_element_type=jnp.float32))
    mixes = []
    for head, scores in enumerate(all_scores):
        scores = jnp.where(causal, scores * scale, -jnp.inf)
        weights = jnp.exp(scores - jnp.max(scores, axis=1, keepdims=True))
        total = jnp.sum(weights, axis=1, keepdims=True)
        mixed = jnp.dot(weights.astype(jnp.bfloat16), v_ref[here, 128 * head:128 * head + 128], preferred_element_type=jnp.float32)
        mixes.append((mixed / total).astype(jnp.bfloat16))
    return jnp.concatenate(mixes, axis=1)


def prefill_kernel(n_heads_steps, n_tiles, x_src, wq_ref, wuk_ref, wuv_ref, lat_src, tab_a, tab_b, tab_c, tab_d, w_ref, cache_src,
                   out_ref, cache_ref, x_ref, lat_ref, q_buf, k_buf, v_buf, heads_out, part, partb, ebuf, ibuf,
                   send_x, recv_x, send_n, recv_n, send_b, recv_p, send_e, recv_e, send_i, recv_i, send_f, send_o, recv_o, local_sem, lat_sem, load_sem):
    step = pl.program_id(0)
    n_chunks = 2 * n_tiles
    t = lax.axis_index("t")
    stage = lax.axis_index("stage")
    is_prompt = stage < 2
    is_relay = stage >= 2
    partner = lax.rem(stage + 2, 4)
    is_end = (t == 0) | (t == 3)
    is_inner = (t == 1) | (t == 2)
    peer = 3 - t
    inner_nb = jnp.where(t == 0, 1, 2)
    end_nb = jnp.where(t == 1, 0, 3)
    pair_nb = jnp.where(is_end, inner_nb, end_nb)
    seq = cache_ref.shape[0]
    prompt_rows = x_ref.shape[0]
    half = seq // 2
    side = lax.rem(t, 2)
    n_pieces = half // PIECE
    drain = step == n_heads_steps + n_tiles
    in_heads = step < n_heads_steps
    in_tiles = (step >= n_heads_steps) & (step < n_heads_steps + n_tiles)

    def tokens_over(p):
        src = pl.multiple_of(prompt_rows + side * half + p * PIECE, PIECE)
        dst = pl.multiple_of(side * half + p * PIECE, PIECE)
        return pltpu.make_async_remote_copy(src_ref=x_src.at[pl.ds(src, PIECE)], dst_ref=x_ref.at[pl.ds(dst, PIECE)], send_sem=send_x.at[p],
                                            recv_sem=recv_x.at[p], device_id={"stage": partner}, device_id_type=MESH)

    def latent_over():
        src = pl.multiple_of(prompt_rows + side * half, half)
        dst = pl.multiple_of(side * half, half)
        return pltpu.make_async_remote_copy(src_ref=lat_src.at[pl.ds(src, half)], dst_ref=lat_ref.at[pl.ds(dst, half)], send_sem=send_x.at[n_pieces],
                                            recv_sem=recv_x.at[n_pieces], device_id={"stage": partner}, device_id_type=MESH)

    def tokens_next(p, which):
        rows = pl.ds(pl.multiple_of(which * half + p * PIECE, PIECE), PIECE)
        return pltpu.make_async_remote_copy(src_ref=x_ref.at[rows], dst_ref=x_ref.at[rows], send_sem=send_n.at[p],
                                            recv_sem=recv_n.at[p], device_id={"t": pair_nb}, device_id_type=MESH)

    def latent_next(which):
        rows = pl.ds(pl.multiple_of(which * half, half), half)
        return pltpu.make_async_remote_copy(src_ref=lat_ref.at[rows], dst_ref=lat_ref.at[rows], send_sem=send_n.at[n_pieces],
                                            recv_sem=recv_n.at[n_pieces], device_id={"t": pair_nb}, device_id_type=MESH)

    def to_partner(tile):
        return pltpu.make_async_remote_copy(src_ref=partb.at[tile], dst_ref=part.at[2 * tile], send_sem=send_b.at[tile], recv_sem=recv_p.at[tile],
                                            device_id={"stage": partner}, device_id_type=MESH)

    def end_to_inner(c):
        return pltpu.make_async_remote_copy(src_ref=part.at[c], dst_ref=ebuf.at[c], send_sem=send_e.at[c], recv_sem=recv_e.at[c],
                                            device_id={"t": inner_nb}, device_id_type=MESH)

    def inner_to_peer(c):
        return pltpu.make_async_remote_copy(src_ref=part.at[c], dst_ref=ibuf.at[c], send_sem=send_i.at[c], recv_sem=recv_i.at[c],
                                            device_id={"t": peer}, device_id_type=MESH)

    def final_to_end(c, src):
        return pltpu.make_async_remote_copy(src_ref=src.at[c], dst_ref=ibuf.at[c], send_sem=send_f.at[c], recv_sem=recv_i.at[c],
                                            device_id={"t": end_nb}, device_id_type=MESH)

    def place(c, line):
        row = (2 * line + lax.rem(c, 2)) * seq
        col = lax.div(c, 2) * TILE
        return out_ref.at[pl.ds(pl.multiple_of(row, seq), seq), pl.ds(pl.multiple_of(col, TILE), TILE)]

    def final_back(c, src):
        return pltpu.make_async_remote_copy(src_ref=src.at[c], dst_ref=place(c, 1), send_sem=send_o.at[c],
                                            recv_sem=recv_o.at[c], device_id={"stage": partner}, device_id_type=MESH)

    def final_local(c, src):
        return pltpu.make_async_copy(src.at[c], place(c, 0), local_sem.at[c])

    def cache_copy():
        return pltpu.make_async_remote_copy(src_ref=cache_src.at[pl.ds(pl.multiple_of(t * seq, seq), seq)], dst_ref=cache_ref, send_sem=lat_sem.at[0],
                                            recv_sem=lat_sem.at[1], device_id={"stage": partner}, device_id_type=MESH)

    def deliver(c, src):
        @pl.when(is_prompt)
        def _():
            final_local(c, src).start()

        @pl.when(is_relay)
        def _():
            final_back(c, src).start()

    @pl.when(step == 0)
    def _():
        barrier = pltpu.get_barrier_semaphore()
        pl.semaphore_signal(barrier, inc=1, device_id={"stage": partner}, device_id_type=MESH)

        @pl.when(is_end)
        def _():
            pl.semaphore_signal(barrier, inc=1, device_id={"t": inner_nb}, device_id_type=MESH)
            pl.semaphore_wait(barrier, 2)

        @pl.when(is_inner)
        def _():
            pl.semaphore_signal(barrier, inc=1, device_id={"t": end_nb}, device_id_type=MESH)
            pl.semaphore_signal(barrier, inc=1, device_id={"t": peer}, device_id_type=MESH)
            pl.semaphore_wait(barrier, 3)

        @pl.when(is_prompt)
        def _():
            load_x = pltpu.make_async_copy(x_src.at[pl.ds(0, prompt_rows)], x_ref, load_sem.at[0])
            load_lat = pltpu.make_async_copy(lat_src.at[pl.ds(0, prompt_rows)], lat_ref, load_sem.at[1])
            load_x.start()
            load_lat.start()

            @pl.loop(0, n_pieces)
            def _(p):
                tokens_over(p).start()

            latent_over().start()
            load_x.wait()
            load_lat.wait()

        @pl.when(is_relay)
        def _():
            @pl.loop(0, n_pieces)
            def _(p):
                tokens_over(p).wait_recv()
                tokens_next(p, side).start()

            latent_over().wait_recv()
            latent_next(side).start()

            @pl.loop(0, n_pieces)
            def _(p):
                tokens_next(p, 1 - side).wait_recv()

            latent_next(1 - side).wait_recv()

    def attend(rows):
        width = HEADS_STEP * V_DIM
        slot = lax.rem(step + 1, 2)
        done = lax.rem(step + n_heads_steps - 1, n_heads_steps)
        for req in range(rows // seq):
            here = slice(req * seq, (req + 1) * seq)
            heads_out[here, pl.ds(pl.multiple_of(done * width, width), width)] = attend_request(
                q_buf.at[slot], k_buf.at[slot], v_buf.at[slot], lat_ref, (tab_a, tab_b, tab_c, tab_d), here, seq)

    for mine, rows in ((is_prompt, prompt_rows), (is_relay, seq)):
        @pl.when(mine & in_heads)
        def _():
            attend(rows)
            project_heads(rows, lax.rem(step, 2), x_ref, wq_ref, wuk_ref, wuv_ref, lat_ref, q_buf, k_buf, v_buf)

        @pl.when(mine & (step == n_heads_steps))
        def _():
            attend(rows)

    @pl.when(is_prompt & (step == n_heads_steps))
    def _():
        cache_copy().start()

    @pl.when(is_prompt & in_tiles)
    def _():
        tile = step - n_heads_steps
        full = jnp.dot(heads_out[...], w_ref[...], preferred_element_type=jnp.float32).astype(jnp.bfloat16)
        part[2 * tile] = full[:seq]
        part[2 * tile + 1] = full[seq:2 * seq]
        partb[tile] = full[2 * seq:]
        to_partner(tile).start()

        @pl.when(is_end)
        def _():
            end_to_inner(2 * tile).start()
            end_to_inner(2 * tile + 1).start()

    @pl.when(is_relay & in_tiles)
    def _():
        c = 2 * (step - n_heads_steps) + 1
        part[c] = jnp.dot(heads_out[:seq], w_ref[...], preferred_element_type=jnp.float32).astype(jnp.bfloat16)

        @pl.when(is_end)
        def _():
            end_to_inner(c).start()

    def tick(tau):
        def live(c):
            return (c >= 0) & (c < n_chunks)

        def root(c):
            return 1 + lax.rem(c + 2 * n_chunks, 2)

        own = tau - jnp.where(is_relay, HOP_LAG, 0)
        arrives = is_relay & (lax.rem(own + 2 * n_chunks, 2) == 0)

        @pl.when(arrives & live(own))
        def _():
            to_partner(lax.div(own, 2)).wait_recv()

            @pl.when(is_end)
            def _():
                end_to_inner(own).start()

        first = own - HOP_LAG

        @pl.when(is_inner & live(first))
        def _():
            end_to_inner(first).wait_recv()

            @pl.when(t != root(first))
            def _():
                part[first] = (part[first].astype(jnp.float32) + ebuf[first].astype(jnp.float32)).astype(jnp.bfloat16)
                inner_to_peer(first).start()

        second = first - HOP_LAG

        @pl.when(is_inner & live(second) & (t == root(second)))
        def _():
            inner_to_peer(second).wait_recv()
            total = part[second].astype(jnp.float32) + ebuf[second].astype(jnp.float32) + ibuf[second].astype(jnp.float32)
            part[second] = total.astype(jnp.bfloat16)
            inner_to_peer(second).start()
            final_to_end(second, part).start()
            deliver(second, part)

        third = second - HOP_LAG

        @pl.when(is_inner & live(third) & (t != root(third)))
        def _():
            inner_to_peer(third).wait_recv()
            final_to_end(third, ibuf).start()
            deliver(third, ibuf)

        fourth = third - HOP_LAG

        @pl.when(is_end & live(fourth))
        def _():
            final_to_end(fourth, ibuf).wait_recv()
            deliver(fourth, ibuf)

    n_ticks = n_chunks + 5 * HOP_LAG

    def ticks_done(at):
        tile = at - n_heads_steps
        return jnp.where(tile < 0, 0, jnp.where(tile < n_tiles, 2 * (tile + 1), n_ticks))

    @pl.loop(ticks_done(step - 1), ticks_done(step))
    def _(tau):
        tick(tau)

    @pl.when(drain)
    def _():
        @pl.loop(0, n_chunks)
        def _(c):
            @pl.when(is_end)
            def _():
                end_to_inner(c).wait_send()

            @pl.when(is_inner)
            def _():
                inner_to_peer(c).wait_send()
                final_to_end(c, part).wait_send()

            @pl.when(is_prompt)
            def _():
                final_local(c, part).wait()
                final_back(c, part).wait_recv()

            @pl.when(is_relay)
            def _():
                final_back(c, part).wait_send()

        @pl.when(is_prompt)
        def _():
            cache_copy().wait_send()
            latent_over().wait_send()

            @pl.loop(0, n_tiles)
            def _(tile):
                to_partner(tile).wait_send()

            @pl.loop(0, n_pieces)
            def _(p):
                tokens_over(p).wait_send()

        @pl.when(is_relay)
        def _():
            cache_copy().wait_recv()
            latent_next(side).wait_send()

            @pl.loop(0, n_pieces)
            def _(p):
                tokens_next(p, side).wait_send()


def prefill(tokens, latent, padded, w_query, w_uk, w_uv, w_out, seq_len):
    rows, width = tokens.shape
    depth = w_out.shape[0]
    kv_rank = w_uk.shape[0]
    n_heads_steps = depth // (HEADS_STEP * V_DIM)
    n_tiles = width // TILE
    prompt_rows = rows - seq_len
    n_pieces = seq_len // 2 // PIECE

    def head_block(i):
        return jnp.minimum(i, n_heads_steps - 1)

    def tile_block(i):
        return jnp.clip(i - n_heads_steps, 0, n_tiles - 1)

    any_spec = pl.BlockSpec(memory_space=pl.ANY)
    tabs = lane_tables(seq_len)
    tab_spec = pl.BlockSpec((seq_len, 128), lambda i: (0, 0))
    chunk = pltpu.VMEM((2 * n_tiles, seq_len, TILE), jnp.bfloat16)
    sems = [n_pieces + 1] * 4 + [n_tiles] * 2 + [2 * n_tiles] * 8 + [2, 2]
    return pl.pallas_call(
        functools.partial(prefill_kernel, n_heads_steps, n_tiles),
        grid=(n_heads_steps + n_tiles + 1,),
        out_shape=(jax.ShapeDtypeStruct((rows, width), jnp.bfloat16), jax.ShapeDtypeStruct((seq_len, latent.shape[1]), jnp.bfloat16)),
        in_specs=[
            any_spec,
            pl.BlockSpec((width, HEADS_STEP * (NOPE_DIM + ROPE_DIM)), lambda i: (0, head_block(i))),
            pl.BlockSpec((kv_rank, HEADS_STEP * NOPE_DIM), lambda i: (0, head_block(i))),
            pl.BlockSpec((kv_rank, HEADS_STEP * V_DIM), lambda i: (0, head_block(i))),
            any_spec,
            tab_spec, tab_spec, tab_spec, tab_spec,
            pl.BlockSpec((depth, TILE), lambda i: (0, tile_block(i))),
            any_spec,
        ],
        out_specs=(any_spec, any_spec),
        scratch_shapes=[
            pltpu.VMEM((prompt_rows, width), jnp.bfloat16),
            pltpu.VMEM((prompt_rows, padded.shape[1]), jnp.bfloat16),
            pltpu.VMEM((2, prompt_rows, HEADS_STEP * (NOPE_DIM + ROPE_DIM)), jnp.bfloat16),
            pltpu.VMEM((2, prompt_rows, HEADS_STEP * NOPE_DIM), jnp.bfloat16),
            pltpu.VMEM((2, prompt_rows, HEADS_STEP * V_DIM), jnp.bfloat16),
            pltpu.VMEM((prompt_rows, depth), jnp.bfloat16),
            chunk,
            pltpu.VMEM((n_tiles, seq_len, TILE), jnp.bfloat16),
            chunk,
            chunk,
        ] + [pltpu.SemaphoreType.DMA((n,)) for n in sems],
        compiler_params=pltpu.CompilerParams(collective_id=0, has_side_effects=True, vmem_limit_bytes=67043328),
    )(tokens, w_query, w_uk, w_uv, padded, *tabs, w_out, latent)


def solution(mesh):
    half_stage = mesh.shape["stage"] // 2
    slot_spec = P(("dp", "stage"), None, None, None)
    cache_spec = P(("dp", "stage"), "t", None, None)

    def device_step(hidden, w_query, w_dkv, latent_gain, w_uk, w_uv, w_out):
        batch, seq_len, width = hidden.shape[1:]
        cos_tab, sin_tab = rope_tables(seq_len)
        latent = latent_rows(hidden[0], w_dkv, latent_gain, cos_tab, sin_tab).reshape(batch * seq_len, -1)
        padded = jnp.pad(latent, ((0, 0), (0, ROPE_DIM)))
        summed, handed = prefill(hidden.reshape(batch * seq_len, width), latent, padded, w_query, w_uk, w_uv, w_out, seq_len)
        is_prompt = lax.axis_index("stage") < half_stage
        out_rows = jnp.where(is_prompt, summed, jnp.zeros_like(summed)).reshape(1, batch, seq_len, width)
        cache = jnp.where(is_prompt, jnp.zeros_like(handed), handed)
        return out_rows, cache[None, None]

    return jax.shard_map(device_step, mesh=mesh, in_specs=(slot_spec, P(None, "t"), P(None, None), P(None), P(None, "t"), P(None, "t"), P("t", None)), out_specs=(slot_spec, cache_spec), check_vma=False)
```

time: 438 us -> 195 us (0.45)
  waiting for transfers between devices: 253 us -> 0 us
  Pallas kernels: 0 us -> 175 us
  matrix products: 116 us -> 8.05 us
  blocking collectives: 18.8 us -> 0 us
  between operations: 14.2 us -> 0.72 us
  local copies, waits for them, and re-layouts: 15.6 us -> 2.83 us
  other arithmetic: 16.6 us -> 7.91 us
    psum x1 -> x0, waiting for transfers between devices: 251 us -> none  [device_step(): summed = lax.psum(part_sum.astype(jnp.bfloat16), 't')]
    pallas_call x0 -> x1, Pallas kernels: none -> 175 us  [prefill(): pl.pallas_call(functools.partial(prefill_kernel, n_heads_steps, n_tiles),...]
    dot_general x7 -> x0, matrix products: 109 us -> none  [the longest x1 52.7 us: attention_partial(): jnp.einsum('bsd,dn->bsn', tokens, w_query, preferred_element_type=jnp.flo...]
    all_gather x1 -> x0, blocking collectives: 18.8 us -> none  [device_step(): all_latent = lax.all_gather(my_latent, 't', axis=0, tiled=True)]
    convert_element_type x1 -> x0, local copies, waits for them, and re-layouts: 8.61 us -> none  [attention_partial(): jnp.einsum('bsd,dn->bsn', tokens, w_query, preferred_element_type=jnp.flo...]
    select_n x0 -> x1, other arithmetic: none -> 6.65 us  [device_step(): jnp.where(is_prompt, summed, jnp.zeros_like(summed))]
    broadcast_in_dim x1, other arithmetic: 6.61 us -> 0.02 us  [device_step(): return (out_rows, cache[None, None])]
    reshape x1 -> x0, local copies, waits for them, and re-layouts: 6.32 us -> none  [attention_partial(): values = values.reshape(batch, seq_len, heads_here, V_DIM)]
  transfers between devices with their start and end apart: 2 -> 0, of which waited for: 2 -> 0; matrix products, arithmetic and copies ran while one was open for 0% -> 0% of each run, Pallas kernels for 0% -> 0%
where the time goes in v2:
time: 195 us
  Pallas kernels  175 us (90%)
  matrix products  8.05 us (4%)
  other arithmetic  7.91 us (4%)
  local copies, waits for them, and re-layouts  2.83 us (1%)
    pallas_call x1, Pallas kernels, prefill(): pl.pallas_call(functools.partial(prefill_kernel, n_heads_steps, n_tiles),...  175 us
    dot_general x1, matrix products, latent_rows(): jnp.einsum('bsd,dc->bsc', tokens, w_dkv, preferred_element_type=jnp.float32)  8.05 us
    select_n x1, other arithmetic, device_step(): jnp.where(is_prompt, summed, jnp.zeros_like(summed))  6.65 us

profile of v2, /device:TPU:0, one launch (start us, length us, event | category | flops | bytes accessed | tf_op | source)
XLA Modules:
  0.0 194.9 jit_solution(3790190275822005794)
XLA Ops:
  0.6 0.7 convert_element_type.20
  1.3 0.1 fusion.12
  1.5 8.1 %fusion.3 = bf16[4,128,576]{1,2,0:T(8,128)(2,1)S(1)} fusion(bf16[7168,576]{0,1:T(8,128)(2,1)} %param.13, bf16[1,4,128,7168]{3,2,1,0:T(8,128)(2,1)} %param.11), kind=kOutput, calls=%fused_computation.4 | convolution fusion | flops 4228153344 | bytes 16187392 | tf_op jit(solution)/shard_map/bsd,dc->bsc/dot_general | solution.py:42
  9.5 0.1 fusion.8
  9.7 0.2 fusion.10
  10.0 0.3 copy.13
  10.3 0.0 copy-start
  10.3 0.8 copy-done
  11.1 0.9 pad.4.lat_src
  12.0 175.3 %shard_map.122 = (bf16[512,7168]{1,0:T(8,128)(2,1)}, bf16[128,576]{1,0:T(8,128)(2,1)}) custom-call(bf16[512,7168]{1,0:T(8,128)(2,1)} %bitcast.16, bf16[7168,6144]{1,0:T(8,128)(2,1)} %wq_ref.1, bf16[512,4096]{1,0:T(8,128)(2,1)} %wuk_ref.1, bf16[512,4096]{1,0:T(8,128)(2,1)} %wuv_ref.1, bf16[512,640]{1,0:T(8,128)(2,1)} %pad.4.lat_src, ...), custom_call_target="tpu_custom_call" | custom-call | tf_op jit(solution)/shard_map/pallas_call | solution.py:422
  187.4 0.0 copy-start.1
  187.4 6.7 %broadcast_select_fusion = bf16[512,7168]{1,0:T(8,128)(2,1)} fusion(bf16[512,7168]{1,0:T(8,128)(2,1)} %get-tuple-element.4, pred[]{:T(512)S(6)} %lt.3), kind=kLoop, calls=%fused_computation.3 | loop fusion | flops 3670016 | bytes 14680065 | tf_op jit(solution)/shard_map/jit(_where)/select_n | solution.py:465
  194.0 0.0 copy-done.1
  194.1 0.8 copy.14
  (6 shorter events, 0.1 us)
Async XLA Ops:
  10.3 0.8 copy-start
  187.4 6.7 %copy-start.1 = (bf16[128,576]{1,0:T(8,128)(2,1)S(1)}, bf16[128,576]{1,0:T(8,128)(2,1)}, u32[]{:S(2)}) copy-start(bf16[128,576]{1,0:T(8,128)(2,1)} %get-tuple-element.5) | copy-start | bytes 442372

commit v3 on v2

v3 whole, which is shorter than its diff:
```python
import functools

import jax
import jax.numpy as jnp
import numpy as np
from jax import lax
from jax.experimental import pallas as pl
from jax.experimental.pallas import tpu as pltpu
from jax.sharding import PartitionSpec as P

NOPE_DIM = 128
ROPE_DIM = 64
V_DIM = 128
NORM_EPS = 1e-6
ROPE_BASE = 10000.0
MESH = pl.DeviceIdType.MESH
TILE = 512
HOP_LAG = 2
HEADS_STEP = 4
PIECE = 16
SHIFTED = 2


def lane_tables(seq_len):
    half_dim = ROPE_DIM // 2
    inv_freq = np.float32(ROPE_BASE) ** (-np.arange(half_dim, dtype=np.float32) / np.float32(half_dim))
    angles = np.arange(seq_len, dtype=np.float32)[:, None] * inv_freq[None, :].astype(np.float32)
    cos_tab, sin_tab = np.cos(angles).astype(np.float32), np.sin(angles).astype(np.float32)
    one, zero = np.ones((seq_len, ROPE_DIM), np.float32), np.zeros((seq_len, ROPE_DIM), np.float32)
    cos_low = np.concatenate([cos_tab, cos_tab, one], axis=1)
    sin_low = np.concatenate([-sin_tab, sin_tab, zero], axis=1)
    cos_high = np.concatenate([one, cos_tab, cos_tab], axis=1)
    sin_high = np.concatenate([zero, -sin_tab, sin_tab], axis=1)
    return cos_low, sin_low, cos_high, sin_high


def rope_lanes(vecs, cos_tab, sin_tab, pick_up):
    as_f32 = vecs.astype(jnp.float32)
    turned = jnp.where(pick_up, pltpu.roll(as_f32, 96, 1), pltpu.roll(as_f32, 32, 1))
    return (as_f32 * cos_tab + turned * sin_tab).astype(jnp.bfloat16)


def project_heads(rows, slot, x_ref, w_buf, wuk_ref, wuv_ref, lat_ref, q_buf, k_buf, v_buf):
    kv_rank = wuk_ref.shape[0]
    q_buf[slot, :rows] = jnp.dot(x_ref[:rows], w_buf[slot], preferred_element_type=jnp.float32).astype(jnp.bfloat16)
    c_kv = lat_ref[:rows, :kv_rank]
    k_buf[slot, :rows] = jnp.dot(c_kv, wuk_ref[...], preferred_element_type=jnp.float32).astype(jnp.bfloat16)
    v_buf[slot, :rows] = jnp.dot(c_kv, wuv_ref[...], preferred_element_type=jnp.float32).astype(jnp.bfloat16)


def latent_heads(rows, x_ref, dkv_ref, gain_ref, cos_low, sin_low, lat_ref, lat_out, seq):
    kv_rank = gain_ref.shape[1]
    compressed = lax.dot_general(x_ref[:rows], dkv_ref[...], (((1,), (1,)), ((), ())), preferred_element_type=jnp.float32).astype(jnp.bfloat16)
    c_raw = compressed[:, :kv_rank].astype(jnp.float32)
    inv_rms = lax.rsqrt(jnp.mean(c_raw * c_raw, axis=1, keepdims=True) + NORM_EPS)
    c_kv = (c_raw * inv_rms * gain_ref[...].astype(jnp.float32)).astype(jnp.bfloat16)
    lat_ref[:rows, :kv_rank] = c_kv
    lat_out[:rows, :kv_rank] = c_kv
    pick_up = (lax.broadcasted_iota(jnp.int32, (seq, 128), 1) & 32) == 0
    wide = jnp.concatenate([compressed[:, kv_rank:], jnp.zeros((rows, ROPE_DIM), jnp.bfloat16)], axis=1)
    for req in range(rows // seq):
        here = slice(req * seq, (req + 1) * seq)
        turned = rope_lanes(wide[here], cos_low[...], sin_low[...], pick_up)
        lat_ref[here, kv_rank:] = turned
        lat_out[here, kv_rank:] = turned[:, :ROPE_DIM]


def attend_request(q_ref, k_ref, v_ref, lat_ref, tabs, here, seq):
    kv_rank = lat_ref.shape[1] - 128
    cos_low, sin_low, cos_high, sin_high = (tab[...] for tab in tabs)
    lane = lax.broadcasted_iota(jnp.int32, (seq, 128), 1)
    low = lane < 64
    pick_up = (lane & 32) == 0
    key_rope = lat_ref[here, kv_rank:]
    key_rope_high = pltpu.roll(key_rope.astype(jnp.float32), 64, 1)
    causal = lax.broadcasted_iota(jnp.int32, (seq, seq), 1) <= lax.broadcasted_iota(jnp.int32, (seq, seq), 0)
    scale = (NOPE_DIM + ROPE_DIM) ** -0.5
    all_scores = []
    for pair in range(HEADS_STEP // 2):
        base = 384 * pair
        q_a = q_ref[here, base:base + 128]
        q_b = rope_lanes(q_ref[here, base + 128:base + 256], cos_low, sin_low, pick_up)
        q_c = rope_lanes(q_ref[here, base + 256:base + 384], cos_high, sin_high, pick_up)
        k_even = k_ref[here, 256 * pair:256 * pair + 128]
        k_odd = pltpu.roll(k_ref[here, 256 * pair + 128:256 * pair + 256].astype(jnp.float32), 64, 1)
        k_odd_a = jnp.where(low, 0.0, k_odd).astype(jnp.bfloat16)
        k_odd_b = jnp.where(low, k_odd, key_rope_high).astype(jnp.bfloat16)
        sides = ((jnp.concatenate([q_a, q_b], axis=1), jnp.concatenate([k_even, key_rope], axis=1)),
                 (jnp.concatenate([q_b, q_c], axis=1), jnp.concatenate([k_odd_a, k_odd_b], axis=1)))
        for q_side, k_side in sides:
            all_scores.append(lax.dot_general(q_side, k_side, (((1,), (1,)), ((), ())), preferred_element_type=jnp.float32))
    mixes = []
    for head, scores in enumerate(all_scores):
        scores = jnp.where(causal, scores * scale, -jnp.inf)
        weights = jnp.exp(scores - jnp.max(scores, axis=1, keepdims=True))
        total = jnp.sum(weights, axis=1, keepdims=True)
        mixed = jnp.dot(weights.astype(jnp.bfloat16), v_ref[here, 128 * head:128 * head + 128], preferred_element_type=jnp.float32)
        mixes.append((mixed / total).astype(jnp.bfloat16))
    return jnp.concatenate(mixes, axis=1)


def prefill_kernel(n_heads_steps, n_tiles, x_src, wq_src, wuk_ref, wuv_ref, gain_ref, tab_a, tab_b, tab_c, tab_d, wout_src, dkv_src,
                   out_ref, cache_ref, x_ref, w_buf, dkv_ref, lat_ref, lat_out, q_buf, k_buf, v_buf, heads_out, part, partb, ebuf, ibuf,
                   send_x, recv_x, send_n, recv_n, send_b, recv_p, send_e, recv_e, send_i, recv_i, send_f, send_o, recv_o, local_sem, lat_sem, load_sem, w_sem):
    step = pl.program_id(0)
    n_line1 = 2 * n_tiles
    n_chunks = n_line1 + SHIFTED
    kept = n_tiles - SHIFTED
    t = lax.axis_index("t")
    stage = lax.axis_index("stage")
    is_prompt = stage < 2
    is_relay = stage >= 2
    partner = lax.rem(stage + 2, 4)
    is_end = (t == 0) | (t == 3)
    is_inner = (t == 1) | (t == 2)
    peer = 3 - t
    inner_nb = jnp.where(t == 0, 1, 2)
    end_nb = jnp.where(t == 1, 0, 3)
    pair_nb = jnp.where(is_end, inner_nb, end_nb)
    seq = cache_ref.shape[0]
    prompt_rows = x_ref.shape[0]
    half = seq // 2
    side = lax.rem(t, 2)
    n_pieces = half // PIECE
    drain = step == n_heads_steps + n_tiles
    in_heads = step < n_heads_steps
    in_tiles = (step >= n_heads_steps) & (step < n_heads_steps + n_tiles)

    def tokens_over(p):
        src = pl.multiple_of(prompt_rows + side * half + p * PIECE, PIECE)
        dst = pl.multiple_of(side * half + p * PIECE, PIECE)
        return pltpu.make_async_remote_copy(src_ref=x_src.at[pl.ds(src, PIECE)], dst_ref=x_ref.at[pl.ds(dst, PIECE)], send_sem=send_x.at[p],
                                            recv_sem=recv_x.at[p], device_id={"stage": partner}, device_id_type=MESH)

    def tokens_next(p, which):
        rows = pl.ds(pl.multiple_of(which * half + p * PIECE, PIECE), PIECE)
        return pltpu.make_async_remote_copy(src_ref=x_ref.at[rows], dst_ref=x_ref.at[rows], send_sem=send_n.at[p],
                                            recv_sem=recv_n.at[p], device_id={"t": pair_nb}, device_id_type=MESH)

    def to_partner(tile):
        return pltpu.make_async_remote_copy(src_ref=partb.at[tile], dst_ref=part.at[2 * tile], send_sem=send_b.at[tile], recv_sem=recv_p.at[tile],
                                            device_id={"stage": partner}, device_id_type=MESH)

    def end_to_inner(c):
        return pltpu.make_async_remote_copy(src_ref=part.at[c], dst_ref=ebuf.at[c], send_sem=send_e.at[c], recv_sem=recv_e.at[c],
                                            device_id={"t": inner_nb}, device_id_type=MESH)

    def inner_to_peer(c):
        return pltpu.make_async_remote_copy(src_ref=part.at[c], dst_ref=ibuf.at[c], send_sem=send_i.at[c], recv_sem=recv_i.at[c],
                                            device_id={"t": peer}, device_id_type=MESH)

    def final_to_end(c):
        return pltpu.make_async_remote_copy(src_ref=ebuf.at[c], dst_ref=ibuf.at[c], send_sem=send_f.at[c], recv_sem=recv_i.at[c],
                                            device_id={"t": end_nb}, device_id_type=MESH)

    def place(c, line):
        extra = c >= n_line1
        row = jnp.where(extra, 2, 2 * line + lax.rem(c, 2)) * seq
        col = jnp.where(extra, kept + c - n_line1, lax.div(c, 2)) * TILE
        return out_ref.at[pl.ds(pl.multiple_of(row, seq), seq), pl.ds(pl.multiple_of(col, TILE), TILE)]

    def final_back(c, src):
        return pltpu.make_async_remote_copy(src_ref=src.at[c], dst_ref=place(c, 1), send_sem=send_o.at[c],
                                            recv_sem=recv_o.at[c], device_id={"stage": partner}, device_id_type=MESH)

    def final_local(c, src):
        return pltpu.make_async_copy(src.at[c], place(c, 0), local_sem.at[c])

    def cache_copy():
        return pltpu.make_async_remote_copy(src_ref=lat_out.at[pl.ds(pl.multiple_of(t * seq, seq), seq)], dst_ref=cache_ref, send_sem=lat_sem.at[0],
                                            recv_sem=lat_sem.at[1], device_id={"stage": partner}, device_id_type=MESH)

    def cache_own():
        return pltpu.make_async_copy(lat_out.at[pl.ds(0, seq)], cache_ref, lat_sem.at[0])

    def on_line(c):
        moved = (c >= 2 * kept) & (lax.rem(c + 2 * n_chunks, 2) == 0)
        return (c >= 0) & ((is_prompt & (c < n_chunks)) | (is_relay & (c < n_line1) & jnp.logical_not(moved)))

    def on_relay_line(c):
        return (c < n_line1) & jnp.logical_not((c >= 2 * kept) & (lax.rem(c, 2) == 0))

    def load_q(i):
        width = w_buf.shape[2]
        return pltpu.make_async_copy(wq_src.at[:, pl.ds(pl.multiple_of(i * width, width), width)], w_buf.at[lax.rem(i, 2)], w_sem.at[lax.rem(i, 2)])

    def load_out(k):
        slot = lax.rem(k + n_heads_steps, 2)
        return pltpu.make_async_copy(wout_src.at[:, pl.ds(pl.multiple_of(k * TILE, TILE), TILE)],
                                     w_buf.at[slot, pl.ds(0, heads_out.shape[1]), pl.ds(0, TILE)], w_sem.at[slot])

    def load_x():
        return pltpu.make_async_copy(x_src.at[pl.ds(0, prompt_rows)], x_ref, load_sem.at[0])

    def load_dkv():
        return pltpu.make_async_copy(dkv_src, dkv_ref, load_sem.at[1])

    def deliver(c, src):
        @pl.when(is_prompt)
        def _():
            final_local(c, src).start()

        @pl.when(is_relay)
        def _():
            final_back(c, src).start()

    @pl.when(step == 0)
    def _():
        @pl.when(is_prompt)
        def _():
            load_x().start()

        load_dkv().start()
        load_q(0).start()
        barrier = pltpu.get_barrier_semaphore()
        pl.semaphore_signal(barrier, inc=1, device_id={"stage": partner}, device_id_type=MESH)

        @pl.when(is_end)
        def _():
            pl.semaphore_signal(barrier, inc=1, device_id={"t": inner_nb}, device_id_type=MESH)
            pl.semaphore_wait(barrier, 2)

        @pl.when(is_inner)
        def _():
            pl.semaphore_signal(barrier, inc=1, device_id={"t": end_nb}, device_id_type=MESH)
            pl.semaphore_signal(barrier, inc=1, device_id={"t": peer}, device_id_type=MESH)
            pl.semaphore_wait(barrier, 3)

        @pl.when(is_prompt)
        def _():
            @pl.loop(0, n_pieces)
            def _(p):
                tokens_over(p).start()

            load_x().wait()
            load_dkv().wait()
            latent_heads(prompt_rows, x_ref, dkv_ref, gain_ref, tab_a, tab_b, lat_ref, lat_out, seq)

        @pl.when(is_relay)
        def _():
            @pl.loop(0, n_pieces)
            def _(p):
                tokens_over(p).wait_recv()
                tokens_next(p, side).start()

            load_dkv().wait()

            @pl.loop(0, n_pieces)
            def _(p):
                tokens_next(p, 1 - side).wait_recv()

            latent_heads(seq, x_ref, dkv_ref, gain_ref, tab_a, tab_b, lat_ref, lat_out, seq)

    @pl.when(step + 1 < n_heads_steps)
    def _():
        load_q(step + 1).start()

    @pl.when((step + 1 >= n_heads_steps) & (step + 1 < n_heads_steps + n_tiles))
    def _():
        load_out(step + 1 - n_heads_steps).start()

    @pl.when(in_heads)
    def _():
        load_q(step).wait()

    @pl.when(in_tiles)
    def _():
        load_out(step - n_heads_steps).wait()

    def attend(rows):
        width = HEADS_STEP * V_DIM
        slot = lax.rem(step + 1, 2)
        done = lax.rem(step + n_heads_steps - 1, n_heads_steps)
        for req in range(rows // seq):
            here = slice(req * seq, (req + 1) * seq)
            heads_out[here, pl.ds(pl.multiple_of(done * width, width), width)] = attend_request(
                q_buf.at[slot], k_buf.at[slot], v_buf.at[slot], lat_ref, (tab_a, tab_b, tab_c, tab_d), here, seq)

    for mine, rows in ((is_prompt, prompt_rows), (is_relay, seq)):
        @pl.when(mine & in_heads)
        def _():
            attend(rows)
            project_heads(rows, lax.rem(step, 2), x_ref, w_buf, wuk_ref, wuv_ref, lat_ref, q_buf, k_buf, v_buf)

        @pl.when(mine & (step == n_heads_steps))
        def _():
            attend(rows)

    @pl.when(is_prompt & (step == n_heads_steps) & (t < 3))
    def _():
        cache_copy().start()

    @pl.when(is_relay & (step == n_heads_steps) & (t == 3))
    def _():
        cache_own().start()

    def out_block():
        return w_buf[lax.rem(step, 2), :heads_out.shape[1], :TILE]

    @pl.when(is_prompt & in_tiles)
    def _():
        tile = step - n_heads_steps
        full = jnp.dot(heads_out[...], out_block(), preferred_element_type=jnp.float32).astype(jnp.bfloat16)
        part[2 * tile] = full[:seq]
        part[2 * tile + 1] = full[seq:2 * seq]

        @pl.when(tile < kept)
        def _():
            partb[tile] = full[2 * seq:]
            to_partner(tile).start()

        @pl.when(tile >= kept)
        def _():
            part[n_line1 + tile - kept] = full[2 * seq:]

        @pl.when(is_end)
        def _():
            end_to_inner(2 * tile).start()
            end_to_inner(2 * tile + 1).start()

            @pl.when(tile >= kept)
            def _():
                end_to_inner(n_line1 + tile - kept).start()

    @pl.when(is_relay & in_tiles)
    def _():
        c = 2 * (step - n_heads_steps) + 1
        part[c] = jnp.dot(heads_out[:seq], out_block(), preferred_element_type=jnp.float32).astype(jnp.bfloat16)

        @pl.when(is_end)
        def _():
            end_to_inner(c).start()

    def tick(tau):
        own = tau - jnp.where(is_relay, HOP_LAG, 0)
        arrives = is_relay & (lax.rem(own + 2 * n_chunks, 2) == 0)

        @pl.when(arrives & on_line(own))
        def _():
            to_partner(lax.div(own, 2)).wait_recv()

            @pl.when(is_end)
            def _():
                end_to_inner(own).start()

        first = own - HOP_LAG

        @pl.when(is_inner & on_line(first))
        def _():
            end_to_inner(first).wait_recv()

            part[first] = (part[first].astype(jnp.float32) + ebuf[first].astype(jnp.float32)).astype(jnp.bfloat16)
            inner_to_peer(first).start()

        second = first - HOP_LAG

        @pl.when(is_inner & on_line(second))
        def _():
            inner_to_peer(second).wait_recv()
            ebuf[second] = (part[second].astype(jnp.float32) + ibuf[second].astype(jnp.float32)).astype(jnp.bfloat16)
            final_to_end(second).start()
            deliver(second, ebuf)

        third = second - HOP_LAG

        @pl.when(is_end & on_line(third))
        def _():
            final_to_end(third).wait_recv()
            deliver(third, ibuf)

    n_ticks = max(n_chunks + 3 * HOP_LAG, n_line1 + 4 * HOP_LAG)

    def ticks_done(at):
        tile = at - n_heads_steps
        return jnp.where(tile < 0, 0, jnp.where(tile < n_tiles, 2 * (tile + 1), n_ticks))

    @pl.loop(ticks_done(step - 1), ticks_done(step))
    def _(tau):
        tick(tau)

    @pl.when(drain)
    def _():
        @pl.loop(0, n_chunks)
        def _(c):
            @pl.when(is_end & on_line(c))
            def _():
                end_to_inner(c).wait_send()

            @pl.when(is_inner & on_line(c))
            def _():
                inner_to_peer(c).wait_send()
                final_to_end(c).wait_send()

            @pl.when(is_prompt)
            def _():
                final_local(c, part).wait()

            @pl.when(is_prompt & on_relay_line(c))
            def _():
                final_back(c, part).wait_recv()

            @pl.when(is_relay & on_line(c))
            def _():
                final_back(c, part).wait_send()

        @pl.when(is_prompt)
        def _():
            @pl.when(t < 3)
            def _():
                cache_copy().wait_send()

            @pl.loop(0, kept)
            def _(tile):
                to_partner(tile).wait_send()

            @pl.loop(0, n_pieces)
            def _(p):
                tokens_over(p).wait_send()

        @pl.when(is_relay)
        def _():
            @pl.when(t < 3)
            def _():
                cache_copy().wait_recv()

            @pl.when(t == 3)
            def _():
                cache_own().wait()

            @pl.loop(0, n_pieces)
            def _(p):
                tokens_next(p, side).wait_send()


def prefill(tokens, w_query, w_dkv, gain, w_uk, w_uv, w_out, seq_len):
    rows, width = tokens.shape
    depth = w_out.shape[0]
    kv_rank = w_uk.shape[0]
    n_heads_steps = depth // (HEADS_STEP * V_DIM)
    n_tiles = width // TILE
    prompt_rows = rows - seq_len
    latent_width = w_dkv.shape[0]
    n_pieces = seq_len // 2 // PIECE

    def head_block(i):
        return jnp.minimum(i, n_heads_steps - 1)

    any_spec = pl.BlockSpec(memory_space=pl.ANY)
    tabs = lane_tables(seq_len)
    tab_spec = pl.BlockSpec((seq_len, 128), lambda i: (0, 0))
    chunk = pltpu.VMEM((2 * n_tiles + SHIFTED, seq_len, TILE), jnp.bfloat16)
    sems = [n_pieces] * 4 + [n_tiles] * 2 + [2 * n_tiles + SHIFTED] * 8 + [2, 2, 2]
    return pl.pallas_call(
        functools.partial(prefill_kernel, n_heads_steps, n_tiles),
        grid=(n_heads_steps + n_tiles + 1,),
        out_shape=(jax.ShapeDtypeStruct((rows, width), jnp.bfloat16), jax.ShapeDtypeStruct((seq_len, latent_width), jnp.bfloat16)),
        in_specs=[
            any_spec,
            any_spec,
            pl.BlockSpec((kv_rank, HEADS_STEP * NOPE_DIM), lambda i: (0, head_block(i))),
            pl.BlockSpec((kv_rank, HEADS_STEP * V_DIM), lambda i: (0, head_block(i))),
            pl.BlockSpec((1, kv_rank), lambda i: (0, 0)),
            tab_spec, tab_spec, tab_spec, tab_spec,
            any_spec,
            any_spec,
        ],
        out_specs=(any_spec, any_spec),
        scratch_shapes=[
            pltpu.VMEM((prompt_rows, width), jnp.bfloat16),
            pltpu.VMEM((2, width, HEADS_STEP * (NOPE_DIM + ROPE_DIM)), jnp.bfloat16),
            pltpu.VMEM((latent_width, width), jnp.bfloat16),
            pltpu.VMEM((prompt_rows, kv_rank + 128), jnp.bfloat16),
            pltpu.VMEM((prompt_rows, latent_width), jnp.bfloat16),
            pltpu.VMEM((2, prompt_rows, HEADS_STEP * (NOPE_DIM + ROPE_DIM)), jnp.bfloat16),
            pltpu.VMEM((2, prompt_rows, HEADS_STEP * NOPE_DIM), jnp.bfloat16),
            pltpu.VMEM((2, prompt_rows, HEADS_STEP * V_DIM), jnp.bfloat16),
            pltpu.VMEM((prompt_rows, depth), jnp.bfloat16),
            chunk,
            pltpu.VMEM((n_tiles, seq_len, TILE), jnp.bfloat16),
            chunk,
            chunk,
        ] + [pltpu.SemaphoreType.DMA((n,)) for n in sems],
        compiler_params=pltpu.CompilerParams(collective_id=0, has_side_effects=True, vmem_limit_bytes=67043328),
    )(tokens, w_query, w_uk, w_uv, gain, *tabs, w_out, w_dkv)


def solution(mesh):
    half_stage = mesh.shape["stage"] // 2
    slot_spec = P(("dp", "stage"), None, None, None)
    cache_spec = P(("dp", "stage"), "t", None, None)

    def device_step(hidden, w_query, w_dkv, latent_gain, w_uk, w_uv, w_out):
        batch, seq_len, width = hidden.shape[1:]
        summed, handed = prefill(hidden.reshape(batch * seq_len, width), w_query, w_dkv.T, latent_gain[None], w_uk, w_uv, w_out, seq_len)
        is_prompt = lax.axis_index("stage") < half_stage
        out_rows = jnp.where(is_prompt, summed, jnp.zeros_like(summed)).reshape(1, batch, seq_len, width)
        cache = jnp.where(is_prompt, jnp.zeros_like(handed), handed)
        return out_rows, cache[None, None]

    return jax.shard_map(device_step, mesh=mesh, in_specs=(slot_spec, P(None, "t"), P(None, None), P(None), P(None, "t"), P(None, "t"), P("t", None)), out_specs=(slot_spec, cache_spec), check_vma=False)
```

time: 195 us -> 178 us (0.913)
  matrix products: 8.05 us -> 0 us
  Pallas kernels: 175 us -> 169 us
    dot_general x1 -> x0, matrix products: 8.05 us -> none  [latent_rows(): jnp.einsum('bsd,dc->bsc', tokens, w_dkv, preferred_element_type=jnp.float32)]
    pallas_call x1, Pallas kernels: 175 us -> 169 us  [prefill(): pl.pallas_call(functools.partial(prefill_kernel, n_heads_steps, n_tiles),...]
where the time goes in v3:
time: 178 us
  Pallas kernels  169 us (95%)
  other arithmetic  6.67 us (4%)
  local copies, waits for them, and re-layouts  2.05 us (1%)
    pallas_call x1, Pallas kernels, prefill(): pl.pallas_call(functools.partial(prefill_kernel, n_heads_steps, n_tiles),...  169 us
    select_n x1, other arithmetic, device_step(): jnp.where(is_prompt, summed, jnp.zeros_like(summed))  6.65 us

profile of v3, /device:TPU:0, one launch (start us, length us, event | category | flops | bytes accessed | tf_op | source)
XLA Modules:
  0.0 178.2 jit_solution(8580248565751428942)
XLA Ops:
  0.6 1.3 broadcast_in_dim.12.gain_ref
  1.9 168.8 %shard_map.122 = (bf16[512,7168]{1,0:T(8,128)(2,1)}, bf16[128,576]{1,0:T(8,128)(2,1)}) custom-call(bf16[512,7168]{1,0:T(8,128)(2,1)} %bitcast.7, bf16[7168,6144]{1,0:T(8,128)(2,1)} %wq_src.1, bf16[512,4096]{1,0:T(8,128)(2,1)} %wuk_ref.1, bf16[512,4096]{1,0:T(8,128)(2,1)} %wuv_ref.1, bf16[1,512]{1,0:T(2,128)(2,1)} %broadcast_in_dim.12.gain_ref, ...), custom_call_target="tpu_custom_call" | custom-call | tf_op jit(solution)/shard_map/pallas_call | solution.py:453
  170.7 0.0 copy-start
  170.7 6.7 %broadcast_select_fusion = bf16[512,7168]{1,0:T(8,128)(2,1)} fusion(bf16[512,7168]{1,0:T(8,128)(2,1)} %get-tuple-element.4, pred[]{:T(512)S(6)} %lt.3), kind=kLoop, calls=%fused_computation | loop fusion | flops 3670016 | bytes 14680065 | tf_op jit(solution)/shard_map/jit(_where)/select_n | solution.py:496
  177.4 0.0 copy-done
  177.4 0.8 copy.13
  (1 shorter events, 0.0 us)
Async XLA Ops:
  170.7 6.7 %copy-start = (bf16[128,576]{1,0:T(8,128)(2,1)S(1)}, bf16[128,576]{1,0:T(8,128)(2,1)}, u32[]{:S(2)}) copy-start(bf16[128,576]{1,0:T(8,128)(2,1)} %get-tuple-element.5) | copy-start | bytes 442372

commit v4 on v3

--- a/solution.py
+++ b/solution.py
@@ -18,7 +18,7 @@
 HOP_LAG = 2
 HEADS_STEP = 4
 PIECE = 16
-SHIFTED = 2
+SHIFTED = 1
 
 
 def lane_tables(seq_len):
@@ -49,11 +49,11 @@
 
 
 def latent_heads(rows, x_ref, dkv_ref, gain_ref, cos_low, sin_low, lat_ref, lat_out, seq):
-    kv_rank = gain_ref.shape[1]
+    kv_rank = gain_ref.shape[0]
     compressed = lax.dot_general(x_ref[:rows], dkv_ref[...], (((1,), (1,)), ((), ())), preferred_element_type=jnp.float32).astype(jnp.bfloat16)
     c_raw = compressed[:, :kv_rank].astype(jnp.float32)
     inv_rms = lax.rsqrt(jnp.mean(c_raw * c_raw, axis=1, keepdims=True) + NORM_EPS)
-    c_kv = (c_raw * inv_rms * gain_ref[...].astype(jnp.float32)).astype(jnp.bfloat16)
+    c_kv = (c_raw * inv_rms * gain_ref[...].astype(jnp.float32)[None, :]).astype(jnp.bfloat16)
     lat_ref[:rows, :kv_rank] = c_kv
     lat_out[:rows, :kv_rank] = c_kv
     pick_up = (lax.broadcasted_iota(jnp.int32, (seq, 128), 1) & 32) == 0
@@ -211,7 +211,6 @@
             load_x().start()
 
         load_dkv().start()
-        load_q(0).start()
         barrier = pltpu.get_barrier_semaphore()
         pl.semaphore_signal(barrier, inc=1, device_id={"stage": partner}, device_id_type=MESH)
 
@@ -234,6 +233,7 @@
 
             load_x().wait()
             load_dkv().wait()
+            load_q(0).start()
             latent_heads(prompt_rows, x_ref, dkv_ref, gain_ref, tab_a, tab_b, lat_ref, lat_out, seq)
 
         @pl.when(is_relay)
@@ -244,6 +244,7 @@
                 tokens_next(p, side).start()
 
             load_dkv().wait()
+            load_q(0).start()
 
             @pl.loop(0, n_pieces)
             def _(p):
@@ -459,7 +460,7 @@
             any_spec,
             pl.BlockSpec((kv_rank, HEADS_STEP * NOPE_DIM), lambda i: (0, head_block(i))),
             pl.BlockSpec((kv_rank, HEADS_STEP * V_DIM), lambda i: (0, head_block(i))),
-            pl.BlockSpec((1, kv_rank), lambda i: (0, 0)),
+            pl.BlockSpec((kv_rank,), lambda i: (0,)),
             tab_spec, tab_spec, tab_spec, tab_spec,
             any_spec,
             any_spec,
@@ -491,7 +492,7 @@
 
     def device_step(hidden, w_query, w_dkv, latent_gain, w_uk, w_uv, w_out):
         batch, seq_len, width = hidden.shape[1:]
-        summed, handed = prefill(hidden.reshape(batch * seq_len, width), w_query, w_dkv.T, latent_gain[None], w_uk, w_uv, w_out, seq_len)
+        summed, handed = prefill(hidden.reshape(batch * seq_len, width), w_query, w_dkv.T, latent_gain, w_uk, w_uv, w_out, seq_len)
         is_prompt = lax.axis_index("stage") < half_stage
         out_rows = jnp.where(is_prompt, summed, jnp.zeros_like(summed)).reshape(1, batch, seq_len, width)
         cache = jnp.where(is_prompt, jnp.zeros_like(handed), handed)

time: 178 us -> 175 us (0.983)
  Pallas kernels: 169 us -> 166 us
    pallas_call x1, Pallas kernels: 169 us -> 166 us  [prefill(): pl.pallas_call(functools.partial(prefill_kernel, n_heads_steps, n_tiles),...]
where the time goes in v4:
time: 175 us
  Pallas kernels  166 us (95%)
  other arithmetic  6.67 us (4%)
    pallas_call x1, Pallas kernels, prefill(): pl.pallas_call(functools.partial(prefill_kernel, n_heads_steps, n_tiles),...  166 us
    select_n x1, other arithmetic, device_step(): jnp.where(is_prompt, summed, jnp.zeros_like(summed))  6.65 us

profile of v4, /device:TPU:0, one launch (start us, length us, event | category | flops | bytes accessed | tf_op | source)
XLA Modules:
  0.0 174.5 jit_solution(12157888765460926986)
XLA Ops:
  0.6 166.4 %shard_map.122 = (bf16[512,7168]{1,0:T(8,128)(2,1)}, bf16[128,576]{1,0:T(8,128)(2,1)}) custom-call(bf16[512,7168]{1,0:T(8,128)(2,1)} %bitcast.7, bf16[7168,6144]{1,0:T(8,128)(2,1)} %wq_src.1, bf16[512,4096]{1,0:T(8,128)(2,1)} %wuk_ref.1, bf16[512,4096]{1,0:T(8,128)(2,1)} %wuv_ref.1, bf16[512]{0:T(512)(128)(2,1)} %gain_ref.1, ...), custom_call_target="tpu_custom_call" | custom-call | tf_op jit(solution)/shard_map/pallas_call | solution.py:454
  167.1 0.0 copy-start
  167.1 6.7 %broadcast_select_fusion = bf16[512,7168]{1,0:T(8,128)(2,1)} fusion(bf16[512,7168]{1,0:T(8,128)(2,1)} %get-tuple-element.4, pred[]{:T(512)S(6)} %lt.3), kind=kLoop, calls=%fused_computation | loop fusion | flops 3670016 | bytes 14680065 | tf_op jit(solution)/shard_map/jit(_where)/select_n | solution.py:497
  173.7 0.0 copy-done
  173.8 0.8 copy.13
  (1 shorter events, 0.0 us)
Async XLA Ops:
  167.1 6.7 %copy-start = (bf16[128,576]{1,0:T(8,128)(2,1)S(1)}, bf16[128,576]{1,0:T(8,128)(2,1)}, u32[]{:S(2)}) copy-start(bf16[128,576]{1,0:T(8,128)(2,1)} %get-tuple-element.5) | copy-start | bytes 442372
